TPU v7x, 32 devices: a whole 2x2x4 slice. The times are simulated.
32 devices in a mesh: freq: 16 (over z, x, core), row: 2 (over y).
Axes of the slice: x: 2, y: 2, z: 4, core: 2. Of those that a mesh axis runs over, the one named last changes fastest.
Arguments:
- reflect_re: float32 [16, 1728, 1728], P('freq', 'row'), may hold values from -0.046875 to 0.046875
- reflect_im: float32 [16, 1728, 1728], P('freq', 'row'), may hold values from -0.046875 to 0.046875
- focus_re: float32 [16, 1728, 32], P('freq', 'row'), may hold values from -6 to 6
- focus_im: float32 [16, 1728, 32], P('freq', 'row'), may hold values from -6 to 6
- first_arrival: int32 [1728, 32], P('row'), may hold values from 4 to 15
Outputs:
- minus_re: float32 [16, 1728, 32], P('freq', 'row')
- minus_im: float32 [16, 1728, 32], P('freq', 'row')
- plus_re: float32 [16, 1728, 32], P('freq', 'row')
- plus_im: float32 [16, 1728, 32], P('freq', 'row')
All inputs are finite; a program needn't handle non-finite values.
Results may differ from a plain program's by a relative error of at most 0.0001.
Values sent between devices are 32-bit elements; how exact they have to be, the bound alone decides.
No kernel may reach another device: no remote copies, remote signals or barrier semaphores. Data moves between devices by JAX's collectives and lax.ppermute only.
A program may use at most 128 MiB of HBM per device.

v0:
```python
import functools
import math

import jax
import jax.numpy as jnp
import numpy as np
from jax import lax
from jax.experimental import pallas as pl
from jax.experimental.pallas import tpu as pltpu
from jax.sharding import PartitionSpec as P

ITERS = 4
VMEM = pltpu.VMEM
LANES = 128


def up(value, unit):
    return -(-value // unit) * unit


def split(value):
    high = value.astype(jnp.bfloat16)
    low = (value - high.astype(jnp.float32)).astype(jnp.bfloat16)
    return high, low


def rows_step(total, unit=16, most=128):
    return max(s for s in range(unit, most + 1, unit) if total % s == 0)


def prepare_body(shards, half, pad, row_ref, re_ref, im_ref, *outs):
    step = re_ref.shape[0]
    first = pl.program_id(0) * step
    rows = pl.ds(pl.multiple_of(first, step), step)
    for me in range(shards):

        @pl.when(row_ref[0] == me)
        def _():
            for part in range(shards):
                start = (me + part) % shards * half
                for which, ref in enumerate((re_ref, im_ref)):
                    piece = ref[:, start : start + half]
                    if pad > half:
                        zeros = jnp.zeros((step, pad - half), jnp.float32)
                        piece = jnp.concatenate([piece, zeros], axis=1)
                    high, low = split(piece)
                    columns = slice(which * pad, (which + 1) * pad)
                    outs[2 * part][rows, columns] = high
                    outs[2 * part + 1][rows, columns] = low


def prepare(row, reflect_re, reflect_im, shards):
    half, full = reflect_re.shape
    pad = up(half, LANES)
    step = rows_step(half)
    shape = jax.ShapeDtypeStruct((half, 2 * pad), jnp.bfloat16)
    block = pl.BlockSpec((step, full), lambda i: (i, 0))
    return pl.pallas_call(
        functools.partial(prepare_body, shards, half, pad),
        grid=(half // step,),
        in_specs=[pl.BlockSpec(memory_space=pltpu.SMEM), block, block],
        out_specs=[pl.BlockSpec(memory_space=VMEM)] * (2 * shards),
        out_shape=[shape] * (2 * shards),
        compiler_params=pltpu.CompilerParams(vmem_limit_bytes=24 << 20),
        cost_estimate=pl.CostEstimate(
            flops=8 * half * full, bytes_accessed=8 * half * full, transcendentals=0
        ),
        name="prepare",
    )(row, reflect_re, reflect_im)


def product_body(sign, points, has_base, has_acc, last, *refs):
    refs = list(refs)
    out_ref, wide = refs[-2], refs[-1]
    u_ref = refs.pop(0)
    groups, per, half = u_ref.shape
    rows = groups * per
    pad = wide.shape[1]
    base_ref = refs.pop(0) if has_base else None
    acc_ref = refs.pop(0) if has_acc else None
    high_ref, low_ref = refs[0], refs[1]
    if pad > half:
        wide[:, pad - LANES :] = jnp.zeros((rows, LANES), jnp.float32)
    for g in range(groups):
        value = u_ref[g]
        if has_base:
            value = value + base_ref[g]
        wide[g * per : (g + 1) * per, :half] = value
    u = wide[...]
    place = lax.broadcasted_iota(jnp.int32, u.shape, 0) % per
    ahead = pltpu.roll(u, rows - points, 0)
    behind = pltpu.roll(u, points, 0)
    turned = jnp.where(place < points, -ahead, behind)
    if sign < 0:
        turned = -turned
    u_high, u_low = split(u)
    t_high, t_low = split(turned)
    high = jnp.concatenate([u_high, t_high], axis=1)
    low = jnp.concatenate([u_low, t_low], axis=1)
    both = jnp.concatenate([high, low], axis=0)
    dims = (((1,), (1,)), ((), ()))
    one = lax.dot_general(both, high_ref[...], dims, preferred_element_type=jnp.float32)
    two = lax.dot_general(high, low_ref[...], dims, preferred_element_type=jnp.float32)
    total = one[:rows] + one[rows:] + two
    if has_acc:
        total = total + acc_ref[...]
    if last:
        for g in range(groups):
            out_ref[g] = total[g * per : (g + 1) * per]
    else:
        out_ref[...] = total


def product(u, base, acc, high, low, sign, points, last):
    groups, per, half = u.shape
    rows = groups * per
    pad = high.shape[1] // 2
    args = [u] + [x for x in (base, acc) if x is not None] + [high, low]
    out = (groups, per, half) if last else (rows, half)
    return pl.pallas_call(
        functools.partial(
            product_body, sign, points, base is not None, acc is not None, last
        ),
        in_specs=[pl.BlockSpec(memory_space=VMEM)] * len(args),
        out_specs=pl.BlockSpec(memory_space=VMEM),
        out_shape=jax.ShapeDtypeStruct(out, jnp.float32),
        scratch_shapes=[pltpu.VMEM((rows, pad), jnp.float32)],
        compiler_params=pltpu.CompilerParams(vmem_limit_bytes=24 << 20),
        cost_estimate=pl.CostEstimate(
            flops=16 * half * half * rows, bytes_accessed=8 * half * pad, transcendentals=0
        ),
        name="product",
    )(*args)


def window_tables(time_count, points):
    angle = 2.0 * np.pi / time_count * np.arange(time_count)
    table = np.concatenate(
        [
            np.repeat(np.cos(angle)[:, None], points, 1),
            np.repeat(-np.sin(angle)[:, None], points, 1),
        ],
        axis=1,
    )
    return np.repeat(table[:, :, None], LANES, 2).astype(np.float32)


def window_body(freqs, points, g_ref, arrival_ref, table_ref, out_ref):
    times = 2 * freqs
    per, length = g_ref.shape[1:]
    middle = times // 4
    for start in range(0, length, LANES):
        size = min(LANES, length - start)
        lanes = slice(start, start + size)
        place = lax.broadcasted_iota(jnp.int32, (per, size), 0)
        side = jnp.where(place < points, 1.0, -1.0).astype(jnp.float32)
        arrival = arrival_ref[:, lanes]

        def tab(t, k):
            return table_ref[t * k % times][:, :size]

        g = []
        for k in range(freqs):
            weight = (1.0 if k == 0 else 2.0) / times
            g.append(g_ref[k][:, lanes] * weight)
        plus, minus = [], []
        for t in range(middle + 1):
            even = functools.reduce(lambda a, b: a + b, [tab(t, k) * g[k] for k in range(0, freqs, 2)])
            odd = functools.reduce(lambda a, b: a + b, [tab(t, k) * g[k] for k in range(1, freqs, 2)])
            scale = 1.0 if t == 0 else 2.0
            near = jnp.where(t < arrival, (even + odd) * scale, 0.0)
            if t == middle:
                plus.append(near)
                minus.append(near)
                continue
            far = jnp.where(times // 2 - t < arrival, (even - odd) * scale, 0.0)
            plus.append(near + far)
            minus.append(near - far)
        for k in range(freqs):
            source = plus if k % 2 == 0 else minus
            out_ref[k, :, lanes] = functools.reduce(
                lambda a, b: a + b, [tab(t, k) * source[t] for t in range(middle + 1)]
            )


def window_small(g, arrival, points):
    freqs = g.shape[0]
    table = jnp.asarray(window_tables(2 * freqs, points))
    return pl.pallas_call(
        functools.partial(window_body, freqs, points),
        in_specs=[pl.BlockSpec(memory_space=VMEM)] * 3,
        out_specs=pl.BlockSpec(memory_space=VMEM),
        out_shape=jax.ShapeDtypeStruct(g.shape, jnp.float32),
        compiler_params=pltpu.CompilerParams(vmem_limit_bytes=8 << 20),
        cost_estimate=pl.CostEstimate(
            flops=2 * freqs * g.size, bytes_accessed=8 * g.size, transcendentals=0
        ),
        name="window",
    )(g, arrival, table)


def window_large(g, arrival, points):
    freqs, per, length = g.shape
    times = 2 * freqs
    highest = lax.Precision.HIGHEST
    count = times // 2 + 1
    angle = 2.0 * np.pi / times * (np.arange(count)[:, None] * np.arange(freqs)[None, :] % times)
    weight = np.where(np.arange(freqs) == 0, 1.0, 2.0) / times
    fold = np.where(np.arange(count) % (times // 2) == 0, 1.0, 2.0)[:, None]
    mask = (jnp.arange(count, dtype=jnp.int32)[:, None, None] < arrival[None, :points]).astype(jnp.float32)
    outs = []
    for basis, part in ((np.cos(angle), g[:, :points]), (-np.sin(angle), g[:, points:])):
        forth = jnp.asarray((basis * weight).astype(np.float32))
        back = jnp.asarray((basis * fold).astype(np.float32))
        traces = jnp.einsum("tk,kil->til", forth, part, precision=highest) * mask
        outs.append(jnp.einsum("tk,til->kil", back, traces, precision=highest))
    return jnp.concatenate(outs, axis=1)


def local(reflect_re, reflect_im, focus_re, focus_im, first_arrival):
    shards = lax.axis_size("row")
    owners = lax.axis_size("freq")
    _, half, count = focus_re.shape
    groups = math.gcd(owners, count)
    points = count // groups
    cuts = owners // groups
    row = lax.axis_index("row")
    owner = lax.axis_index("freq")

    def field(re, im):
        both = jnp.stack([re[0].T.reshape(groups, points, half), im[0].T.reshape(groups, points, half)], axis=1)
        return both.reshape(groups, 2 * points, half)

    def out(value):
        both = value.reshape(groups, 2, points, half)
        return [both[:, c].reshape(count, half).T[None] for c in range(2)]

    def to_owners(value):
        if cuts > 1:
            value = value.reshape(groups, 2 * points, cuts, half // cuts).swapaxes(1, 2)
        value = value.reshape(owners, 2 * points, half // cuts)
        return lax.all_to_all(value, "freq", 0, 0, tiled=True)

    def from_owners(value):
        value = lax.all_to_all(value, "freq", 0, 0, tiled=True)
        if cuts > 1:
            value = value.reshape(groups, cuts, 2 * points, half // cuts).swapaxes(1, 2)
        return value.reshape(groups, 2 * points, half)

    def shift(value, by):
        pairs = [(i, (i - by) % shards) for i in range(shards)]
        return lax.ppermute(value, "row", pairs)

    arrival = first_arrival.T.reshape(groups, points, cuts, half // cuts).swapaxes(1, 2)
    arrival = arrival.reshape(owners, points, half // cuts)
    arrival = lax.dynamic_index_in_dim(arrival, owner, 0, keepdims=False)
    arrival = jnp.concatenate([arrival, arrival], axis=0)
    window = window_small if owners <= 32 else window_large

    base = field(focus_re, focus_im)
    bases = [base] + [shift(base, by) for by in range(1, shards)]
    parts = prepare(row.reshape(1), reflect_re[0], reflect_im[0], shards)

    def apply(fields, adds, sign):
        acc = None
        for by in range(shards):
            add = adds[by] if adds is not None else None
            acc = product(fields[by], add, acc, parts[2 * by], parts[2 * by + 1], sign, points, by == shards - 1)
        return from_owners(window(to_owners(acc), arrival, points))

    fields, adds = bases, None
    minus = plus = None
    for section in range(ITERS):
        result = apply(fields, adds, 1 if section % 2 == 0 else -1)
        if section % 2 == 0:
            minus, adds = result, None
        else:
            plus, adds = result, bases
        if section < ITERS - 1:
            fields = [result] + [shift(result, by) for by in range(1, shards)]
    return tuple(out(minus) + out(plus + base))


def solution(mesh):
    spec = P("freq", "row", None)
    return jax.shard_map(
        local,
        mesh=mesh,
        in_specs=(spec, spec, spec, spec, P("row", None)),
        out_specs=(spec, spec, spec, spec),
        check_vma=False,
    )
```

profile of v0, /device:TPU:0, one launch (start us, length us, event | category | flops | bytes accessed | tf_op | source)
XLA Modules:
  0.0 158.6 jit_solution(13623843776758500933)
XLA Ops:
  0.6 1.0 stack_reshape.7
  1.6 1.0 stack_reshape.6
  2.7 0.2 reshape.20.refs_0_.refs_1_
  2.9 3.1 %collective-permute-start = (f32[16,4,864]{2,1,0:T(4,128)S(1)}, f32[16,4,864]{2,1,0:T(4,128)S(1)}, u32[]{:S(2)}, u32[]{:S(2)}) collective-permute-start(f32[16,4,864]{2,1,0:T(4,128)S(1)} %reshape.20.refs_0_.refs_1_), channel_id=1, source_target_pairs={{0,1},{1,0},{2,3},{3,2},{4,5},{5,4},{6,7},{7,6},{8,9},{9,8},{10,11... | collective-permute-start | bytes 663560 | tf_op jit(solution)/shard_map/ppermute | solution.py:252
  5.9 2.8 %copy-done.6 = f32[1,864,1728]{2,1,0:T(8,128)S(1)} copy-done((f32[1,864,1728]{2,1,0:T(8,128)S(1)}, f32[1,864,1728]{2,1,0:T(8,128)}, u32[]{:S(2)}) %copy-start.6) | copy-done | bytes 5971992
  8.7 2.8 %copy-done.7 = f32[1,864,1728]{2,1,0:T(8,128)S(1)} copy-done((f32[1,864,1728]{2,1,0:T(8,128)S(1)}, f32[1,864,1728]{2,1,0:T(8,128)}, u32[]{:S(2)}) %copy-start.7) | copy-done | bytes 5971992
  11.5 3.3 %prepare.1 = (bf16[864,1792]{1,0:T(8,128)(2,1)S(1)}, bf16[864,1792]{1,0:T(8,128)(2,1)S(1)}, bf16[864,1792]{1,0:T(8,128)(2,1)S(1)}, bf16[864,1792]{1,0:T(8,128)(2,1)S(1)}) custom-call(s32[1]{0:T(128)} %bitcast.6.row_ref, f32[864,1728]{1,0:T(8,128)S(1)} %bitcast.26, f32[864,1728]{1,0:T(8,128)S(1)} %bitcast.27), custom_call_target="tpu_custom_call" | custom-call | flops 11943936 | bytes 11943936 | tf_op jit(solution)/shard_map/prepare/pallas_call | solution.py:58
  14.8 2.0 %product.8.refs_1_ = f32[64,864]{1,0:T(8,128)S(1)} custom-call(f32[16,4,864]{2,1,0:T(4,128)S(1)} %reshape.20.refs_0_.refs_1_, bf16[864,1792]{1,0:T(8,128)(2,1)S(1)} %get-tuple-element.8.refs_1_.refs_2_, bf16[864,1792]{1,0:T(8,128)(2,1)S(1)} %get-tuple-element.9.refs_2_.refs_3_), custom_call_target="tpu_custom_call" | custom-call | flops 764411904 | bytes 6193152 | tf_op jit(solution)/shard_map/product/pallas_call | solution.py:120
  16.8 1.7 %copy-done.4 = bf16[864,1792]{1,0:T(8,128)(2,1)} copy-done((bf16[864,1792]{1,0:T(8,128)(2,1)}, bf16[864,1792]{1,0:T(8,128)(2,1)S(1)}, u32[]{:S(2)}) %copy-start.4) | copy-done | bytes 3096600
  18.5 0.7 copy-done.10
  19.2 0.9 copy-done.11
  20.2 2.0 %product.9 = f32[16,4,864]{2,1,0:T(4,128)S(1)} custom-call(f32[16,4,864]{2,1,0:T(4,128)S(1)} %copy-done.11, f32[64,864]{1,0:T(8,128)S(1)} %product.8.refs_1_, bf16[864,1792]{1,0:T(8,128)(2,1)S(1)} %get-tuple-element.10.refs_2_.refs_3_, bf16[864,1792]{1,0:T(8,128)(2,1)S(1)} %get-tuple-element.11.refs_3_.refs_4_), custom_call_target="tpu_custom_call" | custom-call | flops 764411904 | bytes 6193152 | tf_op jit(solution)/shard_map/product/pallas_call | solution.py:120
  22.1 0.7 copy-done.13
  22.8 5.9 %all-to-all-start = ((f32[16,4,864]{2,1,0:T(4,128)}), f32[16,4,864]{2,1,0:T(4,128)}, u32[]{:S(2)}, u32[]{:S(2)}) async-start(f32[16,4,864]{2,1,0:T(4,128)} %copy-done.13), calls=%async_computation | async-start | bytes 458752 | tf_op jit(solution)/shard_map/all_to_all | solution.py:242
  28.8 1.0 reshape_transpose_reshape.3
  29.8 8.5 %all-to-all-done.g_ref = f32[16,4,864]{2,1,0:T(4,128)} async-done(((f32[16,4,864]{2,1,0:T(4,128)}), f32[16,4,864]{2,1,0:T(4,128)}, u32[]{:S(2)}, u32[]{:S(2)}) %all-to-all-start) | async-done | bytes 221216 | tf_op jit(solution)/shard_map/all_to_all | solution.py:242
  38.3 1.6 window.4
  39.9 12.1 %all_to_all.40.refs_0_ = f32[16,4,864]{2,1,0:T(4,128)S(1)} all-to-all(f32[16,4,864]{2,1,0:T(4,128)S(1)} %window.4), channel_id=1, replica_groups=mesh['freq'=16,'row'=2] {'freq'}, dimensions={0} | all-to-all | bytes 442368 | tf_op jit(solution)/shard_map/all_to_all | solution.py:245
  52.0 0.5 collective-permute-start.1
  52.5 2.1 %copy-done.3 = bf16[864,1792]{1,0:T(8,128)(2,1)S(1)} copy-done((bf16[864,1792]{1,0:T(8,128)(2,1)S(1)}, bf16[864,1792]{1,0:T(8,128)(2,1)}, u32[]{:S(2)}) %copy-start.3) | copy-done | bytes 3096600
  54.6 1.9 %copy-done.5 = bf16[864,1792]{1,0:T(8,128)(2,1)S(1)} copy-done((bf16[864,1792]{1,0:T(8,128)(2,1)S(1)}, bf16[864,1792]{1,0:T(8,128)(2,1)}, u32[]{:S(2)}) %copy-start.5) | copy-done | bytes 3096600
  56.5 2.0 %product.10.refs_1_ = f32[64,864]{1,0:T(8,128)S(1)} custom-call(f32[16,4,864]{2,1,0:T(4,128)S(1)} %all_to_all.40.refs_0_, bf16[864,1792]{1,0:T(8,128)(2,1)S(1)} %copy-done.3, bf16[864,1792]{1,0:T(8,128)(2,1)S(1)} %copy-done.5), custom_call_target="tpu_custom_call" | custom-call | flops 764411904 | bytes 6193152 | tf_op jit(solution)/shard_map/product/pallas_call | solution.py:120
  58.4 0.9 collective-permute-done.1.refs_0_
  59.3 2.0 %product.11 = f32[16,4,864]{2,1,0:T(4,128)S(1)} custom-call(f32[16,4,864]{2,1,0:T(4,128)S(1)} %collective-permute-done.1.refs_0_, f32[64,864]{1,0:T(8,128)S(1)} %product.10.refs_1_, bf16[864,1792]{1,0:T(8,128)(2,1)S(1)} %get-tuple-element.10.refs_2_.refs_3_, bf16[864,1792]{1,0:T(8,128)(2,1)S(1)} %copy-done.1), custom_call_target="tpu_custom_call" | custom-call | flops 764411904 | bytes 6193152 | tf_op jit(solution)/shard_map/product/pallas_call | solution.py:120
  61.3 12.4 %all_to_all.41.g_ref = f32[16,4,864]{2,1,0:T(4,128)S(1)} all-to-all(f32[16,4,864]{2,1,0:T(4,128)S(1)} %product.11), channel_id=1, replica_groups=mesh['freq'=16,'row'=2] {'freq'}, dimensions={0} | all-to-all | bytes 442368 | tf_op jit(solution)/shard_map/all_to_all | solution.py:242
  73.7 0.6 window.5
  74.3 12.1 %all_to_all.42.refs_0_ = f32[16,4,864]{2,1,0:T(4,128)S(1)} all-to-all(f32[16,4,864]{2,1,0:T(4,128)S(1)} %window.5), channel_id=1, replica_groups=mesh['freq'=16,'row'=2] {'freq'}, dimensions={0} | all-to-all | bytes 442368 | tf_op jit(solution)/shard_map/all_to_all | solution.py:245
  86.4 0.5 collective-permute-start.2
  86.9 2.0 %product.12.refs_2_ = f32[64,864]{1,0:T(8,128)S(1)} custom-call(f32[16,4,864]{2,1,0:T(4,128)S(1)} %all_to_all.42.refs_0_, f32[16,4,864]{2,1,0:T(4,128)S(1)} %reshape.20.refs_0_.refs_1_, bf16[864,1792]{1,0:T(8,128)(2,1)S(1)} %copy-done.3, bf16[864,1792]{1,0:T(8,128)(2,1)S(1)} %copy-done.5), custom_call_target="tpu_custom_call" | custom-call | flops 764411904 | bytes 6193152 | tf_op jit(solution)/shard_map/product/pallas_call | solution.py:120
  88.9 4.8 %collective-permute-done.2.refs_0_ = f32[16,4,864]{2,1,0:T(4,128)S(1)} collective-permute-done((f32[16,4,864]{2,1,0:T(4,128)S(1)}, f32[16,4,864]{2,1,0:T(4,128)S(1)}, u32[]{:S(2)}, u32[]{:S(2)}) %collective-permute-start.2) | collective-permute-done | bytes 221216 | tf_op jit(solution)/shard_map/ppermute | solution.py:252
  93.7 2.0 %product.13 = f32[16,4,864]{2,1,0:T(4,128)S(1)} custom-call(f32[16,4,864]{2,1,0:T(4,128)S(1)} %collective-permute-done.2.refs_0_, f32[16,4,864]{2,1,0:T(4,128)S(1)} %copy-done.12, f32[64,864]{1,0:T(8,128)S(1)} %product.12.refs_2_, bf16[864,1792]{1,0:T(8,128)(2,1)S(1)} %get-tuple-element.10.refs_2_.refs_3_, bf16[864,1792]{1,0:T(8,128)(2,1)S(1)} %copy-done.1), custom_call_target="tpu_custom_call" | custom-call | flops 764411904 | bytes 6193152 | tf_op jit(solution)/shard_map/product/pallas_call | solution.py:120
  95.7 12.4 %all_to_all.43.g_ref = f32[16,4,864]{2,1,0:T(4,128)S(1)} all-to-all(f32[16,4,864]{2,1,0:T(4,128)S(1)} %product.13), channel_id=1, replica_groups=mesh['freq'=16,'row'=2] {'freq'}, dimensions={0} | all-to-all | bytes 442368 | tf_op jit(solution)/shard_map/all_to_all | solution.py:242
  108.1 0.6 window.6
  108.8 12.1 %all_to_all.44.refs_0_ = f32[16,4,864]{2,1,0:T(4,128)S(1)} all-to-all(f32[16,4,864]{2,1,0:T(4,128)S(1)} %window.6), channel_id=1, replica_groups=mesh['freq'=16,'row'=2] {'freq'}, dimensions={0} | all-to-all | bytes 442368 | tf_op jit(solution)/shard_map/all_to_all | solution.py:245
  120.8 0.5 collective-permute-start.3
  121.3 2.0 %product.14.refs_1_ = f32[64,864]{1,0:T(8,128)S(1)} custom-call(f32[16,4,864]{2,1,0:T(4,128)S(1)} %all_to_all.44.refs_0_, bf16[864,1792]{1,0:T(8,128)(2,1)S(1)} %copy-done.3, bf16[864,1792]{1,0:T(8,128)(2,1)S(1)} %copy-done.5), custom_call_target="tpu_custom_call" | custom-call | flops 764411904 | bytes 6193152 | tf_op jit(solution)/shard_map/product/pallas_call | solution.py:120
  123.3 4.8 %collective-permute-done.3.refs_0_ = f32[16,4,864]{2,1,0:T(4,128)S(1)} collective-permute-done((f32[16,4,864]{2,1,0:T(4,128)S(1)}, f32[16,4,864]{2,1,0:T(4,128)S(1)}, u32[]{:S(2)}, u32[]{:S(2)}) %collective-permute-start.3) | collective-permute-done | bytes 221216 | tf_op jit(solution)/shard_map/ppermute | solution.py:252
  128.2 2.0 %product.15 = f32[16,4,864]{2,1,0:T(4,128)S(1)} custom-call(f32[16,4,864]{2,1,0:T(4,128)S(1)} %collective-permute-done.3.refs_0_, f32[64,864]{1,0:T(8,128)S(1)} %product.14.refs_1_, bf16[864,1792]{1,0:T(8,128)(2,1)S(1)} %get-tuple-element.10.refs_2_.refs_3_, bf16[864,1792]{1,0:T(8,128)(2,1)S(1)} %copy-done.1), custom_call_target="tpu_custom_call" | custom-call | flops 764411904 | bytes 6193152 | tf_op jit(solution)/shard_map/product/pallas_call | solution.py:120
  130.1 12.4 %all_to_all.45.g_ref = f32[16,4,864]{2,1,0:T(4,128)S(1)} all-to-all(f32[16,4,864]{2,1,0:T(4,128)S(1)} %product.15), channel_id=1, replica_groups=mesh['freq'=16,'row'=2] {'freq'}, dimensions={0} | all-to-all | bytes 442368 | tf_op jit(solution)/shard_map/all_to_all | solution.py:242
  142.6 1.3 window.7
  143.9 3.5 %all-to-all-start.7 = ((f32[16,4,864]{2,1,0:T(4,128)}), f32[16,4,864]{2,1,0:T(4,128)S(1)}, u32[]{:S(2)}, u32[]{:S(2)}) async-start(f32[16,4,864]{2,1,0:T(4,128)} %window.7), calls=%async_computation.7 | async-start | bytes 458752 | tf_op jit(solution)/shard_map/all_to_all | solution.py:245
  147.4 0.2 reshape.22
  147.7 0.7 reshape_squeeze.12
  148.4 0.7 reshape_squeeze.13
  149.1 7.8 %all-to-all-done.7 = f32[16,4,864]{2,1,0:T(4,128)S(1)} async-done(((f32[16,4,864]{2,1,0:T(4,128)}), f32[16,4,864]{2,1,0:T(4,128)S(1)}, u32[]{:S(2)}, u32[]{:S(2)}) %all-to-all-start.7) | async-done | bytes 221216 | tf_op jit(solution)/shard_map/all_to_all | solution.py:245
  157.0 0.2 reshape.23
  157.2 0.7 reshape_squeeze.14
  157.9 0.7 reshape_squeeze.15
  (31 shorter events, 0.3 us)
Async XLA Ops:
  2.9 15.6 %collective-permute-start = (f32[16,4,864]{2,1,0:T(4,128)S(1)}, f32[16,4,864]{2,1,0:T(4,128)S(1)}, u32[]{:S(2)}, u32[]{:S(2)}) collective-permute-start(f32[16,4,864]{2,1,0:T(4,128)S(1)} %reshape.20.refs_0_.refs_1_), channel_id=1, source_target_pairs={{0,1},{1,0},{2,3},{3,2},{4,5},{5,4},{6,7},{7,6},{8,9},{9,8},{10,11... | collective-permute-start | bytes 663560 | tf_op jit(solution)/shard_map/ppermute | solution.py:252
  5.9 2.8 %copy-start.6 = (f32[1,864,1728]{2,1,0:T(8,128)S(1)}, f32[1,864,1728]{2,1,0:T(8,128)}, u32[]{:S(2)}) copy-start(f32[1,864,1728]{2,1,0:T(8,128)} %param.9) | copy-start | bytes 17915908
  8.7 2.8 %copy-start.7 = (f32[1,864,1728]{2,1,0:T(8,128)S(1)}, f32[1,864,1728]{2,1,0:T(8,128)}, u32[]{:S(2)}) copy-start(f32[1,864,1728]{2,1,0:T(8,128)} %param.10) | copy-start | bytes 17915908
  14.8 2.0 %copy-start.2 = (bf16[864,1792]{1,0:T(8,128)(2,1)}, bf16[864,1792]{1,0:T(8,128)(2,1)S(1)}, u32[]{:S(2)}) copy-start(bf16[864,1792]{1,0:T(8,128)(2,1)S(1)} %get-tuple-element.8.refs_1_.refs_2_) | copy-start | bytes 9289732
  14.8 4.4 %copy-start = (bf16[864,1792]{1,0:T(8,128)(2,1)}, bf16[864,1792]{1,0:T(8,128)(2,1)S(1)}, u32[]{:S(2)}) copy-start(bf16[864,1792]{1,0:T(8,128)(2,1)S(1)} %get-tuple-element.11.refs_3_.refs_4_) | copy-start | bytes 9289732
  16.8 1.7 %copy-start.4 = (bf16[864,1792]{1,0:T(8,128)(2,1)}, bf16[864,1792]{1,0:T(8,128)(2,1)S(1)}, u32[]{:S(2)}) copy-start(bf16[864,1792]{1,0:T(8,128)(2,1)S(1)} %get-tuple-element.9.refs_2_.refs_3_) | copy-start | bytes 9289732
  18.5 0.7 copy-start.10
  19.2 0.9 copy-start.11
  20.2 18.2 %copy-start.8 = (f32[32,4,128]{2,1,0:T(4,128)S(1)}, f32[32,4,128]{2,1,0:T(4,128)}, u32[]{:S(2)}) copy-start(f32[32,4,128]{2,1,0:T(4,128)} %constant.16.clone.table_ref) | copy-start | bytes 196612
  22.1 0.7 copy-start.13
  22.8 15.5 %all-to-all-start = ((f32[16,4,864]{2,1,0:T(4,128)}), f32[16,4,864]{2,1,0:T(4,128)}, u32[]{:S(2)}, u32[]{:S(2)}) async-start(f32[16,4,864]{2,1,0:T(4,128)} %copy-done.13), calls=%async_computation | async-start | bytes 458752 | tf_op jit(solution)/shard_map/all_to_all | solution.py:242
  29.8 78.3 %copy-start.14 = (s32[4,864]{1,0:T(4,128)}, s32[4,864]{1,0:T(4,128)S(1)}, u32[]{:S(2)}) copy-start(s32[4,864]{1,0:T(4,128)S(1)} %pad_add_fusion.arrival_ref) | copy-start | bytes 41476
  52.0 7.3 %copy-start.1 = (bf16[864,1792]{1,0:T(8,128)(2,1)S(1)}, bf16[864,1792]{1,0:T(8,128)(2,1)}, u32[]{:S(2)}) copy-start(bf16[864,1792]{1,0:T(8,128)(2,1)} %copy-done) | copy-start | bytes 9289732
  52.0 7.3 %collective-permute-start.1 = (f32[16,4,864]{2,1,0:T(4,128)S(1)}, f32[16,4,864]{2,1,0:T(4,128)S(1)}, u32[]{:S(2)}, u32[]{:S(2)}) collective-permute-start(f32[16,4,864]{2,1,0:T(4,128)S(1)} %all_to_all.40.refs_0_), channel_id=1, source_target_pairs={{0,1},{1,0},{2,3},{3,2},{4,5},{5,4},{6,7},{7,6},{8,9},{9,8},{10,11... | collective-permute-start | bytes 663560 | tf_op jit(solution)/shard_map/ppermute | solution.py:252
  52.5 2.1 %copy-start.3 = (bf16[864,1792]{1,0:T(8,128)(2,1)S(1)}, bf16[864,1792]{1,0:T(8,128)(2,1)}, u32[]{:S(2)}) copy-start(bf16[864,1792]{1,0:T(8,128)(2,1)} %copy-done.2) | copy-start | bytes 9289732
  54.6 1.9 %copy-start.5 = (bf16[864,1792]{1,0:T(8,128)(2,1)S(1)}, bf16[864,1792]{1,0:T(8,128)(2,1)}, u32[]{:S(2)}) copy-start(bf16[864,1792]{1,0:T(8,128)(2,1)} %copy-done.4) | copy-start | bytes 9289732
  86.4 7.3 %copy-start.12 = (f32[16,4,864]{2,1,0:T(4,128)S(1)}, f32[16,4,864]{2,1,0:T(4,128)}, u32[]{:S(2)}) copy-start(f32[16,4,864]{2,1,0:T(4,128)} %copy-done.10) | copy-start | bytes 663556
  86.4 7.3 %collective-permute-start.2 = (f32[16,4,864]{2,1,0:T(4,128)S(1)}, f32[16,4,864]{2,1,0:T(4,128)S(1)}, u32[]{:S(2)}, u32[]{:S(2)}) collective-permute-start(f32[16,4,864]{2,1,0:T(4,128)S(1)} %all_to_all.42.refs_0_), channel_id=1, source_target_pairs={{0,1},{1,0},{2,3},{3,2},{4,5},{5,4},{6,7},{7,6},{8,9},{9,8},{10,11... | collective-permute-start | bytes 663560 | tf_op jit(solution)/shard_map/ppermute | solution.py:252
  120.8 7.3 %collective-permute-start.3 = (f32[16,4,864]{2,1,0:T(4,128)S(1)}, f32[16,4,864]{2,1,0:T(4,128)S(1)}, u32[]{:S(2)}, u32[]{:S(2)}) collective-permute-start(f32[16,4,864]{2,1,0:T(4,128)S(1)} %all_to_all.44.refs_0_), channel_id=1, source_target_pairs={{0,1},{1,0},{2,3},{3,2},{4,5},{5,4},{6,7},{7,6},{8,9},{9,8},{10,11... | collective-permute-start | bytes 663560 | tf_op jit(solution)/shard_map/ppermute | solution.py:252
  123.3 19.3 %copy-start.9 = (f32[32,4,128]{2,1,0:T(4,128)S(1)}, f32[32,4,128]{2,1,0:T(4,128)}, u32[]{:S(2)}) copy-start(f32[32,4,128]{2,1,0:T(4,128)} %constant.16.clone.table_ref) | copy-start | bytes 196612
  123.3 19.3 %copy-start.15 = (s32[4,864]{1,0:T(4,128)S(1)}, s32[4,864]{1,0:T(4,128)}, u32[]{:S(2)}) copy-start(s32[4,864]{1,0:T(4,128)} %copy-done.14) | copy-start | bytes 41476
  143.9 13.0 %all-to-all-start.7 = ((f32[16,4,864]{2,1,0:T(4,128)}), f32[16,4,864]{2,1,0:T(4,128)S(1)}, u32[]{:S(2)}, u32[]{:S(2)}) async-start(f32[16,4,864]{2,1,0:T(4,128)} %window.7), calls=%async_computation.7 | async-start | bytes 458752 | tf_op jit(solution)/shard_map/all_to_all | solution.py:245
where the time goes:
time: 159 us
  blocking collectives  73.5 us (46%)
  waiting for transfers between devices  26.8 us (17%)
  Pallas kernels  23.2 us (15%)
  local copies, waits for them, and re-layouts  20 us (13%)
  starting transfers between devices  14 us (9%)
    all_to_all x3, blocking collectives, to_owners(): return lax.all_to_all(value, 'freq', 0, 0, tiled=True)  37.3 us
    all_to_all x3, blocking collectives, from_owners(): value = lax.all_to_all(value, 'freq', 0, 0, tiled=True)  36.3 us
    pallas_call x8, Pallas kernels, product(): pl.pallas_call(functools.partial(product_body, sign, points, base is not...  15.8 us
    unnamed x32, local copies, waits for them, and re-layouts  13.6 us
    ppermute x4, waiting for transfers between devices, shift(): return lax.ppermute(value, 'row', pairs)  10.5 us
    all_to_all x1, waiting for transfers between devices, to_owners(): return lax.all_to_all(value, 'freq', 0, 0, tiled=True)  8.53 us
    all_to_all x1, waiting for transfers between devices, from_owners(): value = lax.all_to_all(value, 'freq', 0, 0, tiled=True)  7.77 us
    all_to_all x1, starting transfers between devices, to_owners(): return lax.all_to_all(value, 'freq', 0, 0, tiled=True)  5.95 us
  transfers between devices with their start and end apart: 6, of which 5 were waited for; matrix products, arithmetic and copies ran while one was open for 2% of the time, Pallas kernels for 7%

commit v1 on v0

v1 whole, which is shorter than its diff:
```python
import functools
import math

import jax
import jax.numpy as jnp
import numpy as np
from jax import lax
from jax.experimental import pallas as pl
from jax.experimental.pallas import tpu as pltpu
from jax.sharding import PartitionSpec as P

ITERS = 4
VMEM = pltpu.VMEM
SMEM = pltpu.SMEM
LANES = 128


def up(value, unit):
    return -(-value // unit) * unit


def whole(space):
    return pl.BlockSpec(memory_space=space)


def split(value):
    high = value.astype(jnp.bfloat16)
    low = (value - high.astype(jnp.float32)).astype(jnp.bfloat16)
    return high, low


def prepare_body(bands, groups, row_ref, owner_ref, arrival_ref, *refs):
    re_ref, im_ref, high_ref, low_ref, own_ref, re_held, im_held, arrived = refs
    full = re_ref.shape[1]
    pairs = ((re_ref, re_held), (im_ref, im_held))
    copies = {}
    for at, (start, size) in enumerate(bands):
        for which, (source, held) in enumerate(pairs):
            rows = slice(start, start + size)
            copies[at, which] = pltpu.make_async_copy(
                source.at[rows], held.at[rows], arrived.at[at, which]
            )
            copies[at, which].start()
    points = own_ref.shape[0] // 2
    own = jnp.zeros(own_ref.shape, jnp.int32)
    for g in range(groups):
        mine = arrival_ref[g * points : (g + 1) * points]
        own = jnp.where(owner_ref[0] == g, jnp.concatenate([mine, mine], axis=0), own)
    own_ref[...] = own
    for at, (start, size) in enumerate(bands):
        for which, (_, held) in enumerate(pairs):
            copies[at, which].wait()
            for column in range(0, full, LANES):
                width = min(LANES, full - column)
                piece = held[start : start + size, column : column + width]
                high, low = split(piece.T)
                rows = slice(which * full + column, which * full + column + width)
                high_ref[rows, start : start + size] = high
                low_ref[rows, start : start + size] = low


def prepare(row, owner, arrival, reflect_re, reflect_im, groups):
    half, full = reflect_re.shape
    points = arrival.shape[0] // groups
    bands = [(start, min(LANES, half - start)) for start in range(0, half, LANES)]
    shape = jax.ShapeDtypeStruct((2 * full, half), jnp.bfloat16)
    return pl.pallas_call(
        functools.partial(prepare_body, bands, groups),
        in_specs=[whole(SMEM)] * 2 + [whole(VMEM)] + [whole(pltpu.HBM)] * 2,
        out_specs=[whole(VMEM)] * 3,
        out_shape=[shape] * 2 + [jax.ShapeDtypeStruct((2 * points, half), jnp.int32)],
        scratch_shapes=[
            pltpu.VMEM((half, full), jnp.float32),
            pltpu.VMEM((half, full), jnp.float32),
            pltpu.SemaphoreType.DMA((len(bands), 2)),
        ],
        compiler_params=pltpu.CompilerParams(vmem_limit_bytes=40 << 20),
        cost_estimate=pl.CostEstimate(
            flops=32 * half * full * LANES, bytes_accessed=8 * half * full, transcendentals=0
        ),
        name="prepare",
    )(row, owner, arrival, reflect_re, reflect_im)


def product_body(sign, points, shards, joined, adds, emits, *refs):
    refs = list(refs)
    row = refs.pop(0)[0]
    wide = refs.pop()
    field_ref = refs.pop(0) if joined else None
    bases = [refs.pop(0) for _ in range(2 * shards)] if adds else None
    high_ref, low_ref, out_ref = refs[:3]
    groups, per, half = out_ref.shape
    rows = groups * per
    full = shards * half

    def base(rows_in, place, part):
        chosen = bases[part][rows_in]
        for by in range(1, shards):
            here = (row + by) % shards == place
            chosen = jnp.where(here, bases[2 * by + part][rows_in], chosen)
        return chosen

    for g in range(groups):
        rows_in = slice(g * points, (g + 1) * points)
        for place in range(shards):
            value = None
            if adds:
                value = jnp.concatenate([base(rows_in, place, part) for part in range(2)], axis=0)
            if joined:
                field = field_ref[g * shards + place]
                value = field if value is None else field + value
            wide[g * per : (g + 1) * per, place * half : (place + 1) * half] = value
    if emits:
        for g in range(groups):
            value = field_ref[g * shards + row]
            rows_out = slice(g * points, (g + 1) * points)
            refs[3][rows_out] = value[:points]
            refs[4][rows_out] = value[points:]
    u = wide[...]
    place = lax.broadcasted_iota(jnp.int32, u.shape, 0) % per
    ahead = pltpu.roll(u, rows - points, 0)
    behind = pltpu.roll(u, points, 0)
    turned = jnp.where(place < points, -ahead, behind)
    if sign < 0:
        turned = -turned
    u_high, u_low = split(u)
    t_high, t_low = split(turned)

    def times(left, ref, start):
        return lax.dot_general(
            left,
            ref[start : start + full],
            (((1,), (0,)), ((), ())),
            preferred_element_type=jnp.float32,
        )

    one = times(jnp.concatenate([u_high, u_low], axis=0), high_ref, 0)
    one = one + times(jnp.concatenate([t_high, t_low], axis=0), high_ref, full)
    two = times(u_high, low_ref, 0) + times(t_high, low_ref, full)
    result = one[:rows] + one[rows:] + two
    for g in range(groups):
        out_ref[g] = result[g * per : (g + 1) * per, :half]


def product(row, field, bases, high, low, sign, points, groups, shards, emits):
    half = high.shape[1]
    rows = 2 * points * groups
    args = [row] + ([] if field is None else [field]) + bases + [high, low]
    shapes = [jax.ShapeDtypeStruct((groups, 2 * points, half), jnp.float32)]
    if emits:
        shapes += [jax.ShapeDtypeStruct((groups * points, half), jnp.float32)] * 2
    return pl.pallas_call(
        functools.partial(
            product_body, sign, points, shards, field is not None, bool(bases), emits
        ),
        in_specs=[whole(SMEM)] + [whole(VMEM)] * (len(args) - 1),
        out_specs=[whole(VMEM)] * len(shapes),
        out_shape=shapes,
        scratch_shapes=[pltpu.VMEM((rows, shards * half), jnp.float32)],
        compiler_params=pltpu.CompilerParams(vmem_limit_bytes=24 << 20),
        cost_estimate=pl.CostEstimate(
            flops=12 * rows * shards * half * half,
            bytes_accessed=8 * half * half * shards,
            transcendentals=0,
        ),
        name="product",
    )(*args)


def window_tables(time_count, points):
    angle = 2.0 * np.pi / time_count * np.arange(time_count)
    table = np.concatenate(
        [
            np.repeat(np.cos(angle)[:, None], points, 1),
            np.repeat(-np.sin(angle)[:, None], points, 1),
        ],
        axis=1,
    )
    return np.repeat(table[:, :, None], LANES, 2).astype(np.float32)


def add_all(values):
    return functools.reduce(lambda a, b: a + b, values)


def window_body(freqs, points, copies, g_ref, arrival_ref, table_ref, out_ref):
    times = 2 * freqs
    length = g_ref.shape[2]
    middle = times // 4
    for start in range(0, length, LANES):
        size = min(LANES, length - start)
        lanes = slice(start, start + size)
        arrival = arrival_ref[:, lanes]

        def tab(t, k):
            return table_ref[t * k % times][:, :size]

        g = []
        for k in range(freqs):
            weight = (1.0 if k == 0 else 2.0) / times
            g.append(g_ref[k][:, lanes] * weight)
        plus, minus = [], []
        for t in range(middle + 1):
            even = add_all([tab(t, k) * g[k] for k in range(0, freqs, 2)])
            odd = add_all([tab(t, k) * g[k] for k in range(1, freqs, 2)])
            scale = 1.0 if t == 0 else 2.0
            near = jnp.where(t < arrival, (even + odd) * scale, 0.0)
            if t == middle:
                plus.append(near)
                minus.append(near)
                continue
            far = jnp.where(times // 2 - t < arrival, (even - odd) * scale, 0.0)
            plus.append(near + far)
            minus.append(near - far)
        for k in range(freqs):
            source = plus if k % 2 == 0 else minus
            value = add_all([tab(t, k) * source[t] for t in range(middle + 1)])
            for copy in range(copies):
                out_ref[k * copies + copy, :, lanes] = value


def window_small(g, arrival, points, copies):
    freqs = g.shape[0]
    table = jnp.asarray(window_tables(2 * freqs, points))
    return pl.pallas_call(
        functools.partial(window_body, freqs, points, copies),
        in_specs=[whole(VMEM)] * 3,
        out_specs=whole(VMEM),
        out_shape=jax.ShapeDtypeStruct((freqs * copies,) + g.shape[1:], jnp.float32),
        compiler_params=pltpu.CompilerParams(vmem_limit_bytes=8 << 20),
        cost_estimate=pl.CostEstimate(
            flops=2 * freqs * g.size, bytes_accessed=8 * g.size, transcendentals=0
        ),
        name="window",
    )(g, arrival, table)


def window_large(g, arrival, points, copies):
    freqs = g.shape[0]
    times = 2 * freqs
    highest = lax.Precision.HIGHEST
    count = times // 2 + 1
    angle = 2.0 * np.pi / times * (np.arange(count)[:, None] * np.arange(freqs)[None, :] % times)
    weight = np.where(np.arange(freqs) == 0, 1.0, 2.0) / times
    fold = np.where(np.arange(count) % (times // 2) == 0, 1.0, 2.0)[:, None]
    steps = jnp.arange(count, dtype=jnp.int32)[:, None, None]
    mask = (steps < arrival[None, :points]).astype(jnp.float32)
    outs = []
    for basis, part in ((np.cos(angle), g[:, :points]), (-np.sin(angle), g[:, points:])):
        forth = jnp.asarray((basis * weight).astype(np.float32))
        back = jnp.asarray((basis * fold).astype(np.float32))
        traces = jnp.einsum("tk,kil->til", forth, part, precision=highest) * mask
        outs.append(jnp.einsum("tk,til->kil", back, traces, precision=highest))
    return jnp.repeat(jnp.concatenate(outs, axis=1), copies, axis=0)


def finish_body(points, value_ref, base_re_ref, base_im_ref, re_ref, im_ref):
    for g in range(value_ref.shape[0]):
        value = value_ref[g]
        rows = slice(g * points, (g + 1) * points)
        re_ref[rows] = value[:points] + base_re_ref[rows]
        im_ref[rows] = value[points:] + base_im_ref[rows]


def finish(value, base_re, base_im):
    points = value.shape[1] // 2
    return pl.pallas_call(
        functools.partial(finish_body, points),
        in_specs=[whole(VMEM)] * 3,
        out_specs=[whole(VMEM)] * 2,
        out_shape=[jax.ShapeDtypeStruct(base_re.shape, jnp.float32)] * 2,
        compiler_params=pltpu.CompilerParams(vmem_limit_bytes=8 << 20),
        name="finish",
    )(value, base_re, base_im)


def local(reflect_re, reflect_im, focus_re, focus_im, first_arrival):
    shards = lax.axis_size("row")
    owners = lax.axis_size("freq")
    _, half, count = focus_re.shape
    groups = math.gcd(owners, count)
    points = count // groups
    cuts = owners // groups
    row = lax.axis_index("row").reshape(1)
    owner = lax.axis_index("freq").reshape(1)

    def to_owners(value):
        if cuts > 1:
            value = value.reshape(groups, 2 * points, cuts, half // cuts).swapaxes(1, 2)
            value = value.reshape(owners, 2 * points, half // cuts)
        return lax.all_to_all(value, "freq", 0, 0, tiled=True)

    def from_owners(value, axes, copies):
        value = lax.all_to_all(value, axes, 0, 0, tiled=True)
        if cuts > 1:
            value = value.reshape(groups, cuts, copies, 2 * points, half // cuts)
            value = value.transpose(0, 2, 3, 1, 4)
        return value.reshape(groups * copies, 2 * points, half)

    def shift(value, by):
        return lax.ppermute(value, "row", [(i, (i - by) % shards) for i in range(shards)])

    window = window_small if owners <= 32 else window_large
    bases = [focus_re[0].T, focus_im[0].T]
    for by in range(1, shards):
        bases += [shift(part, by) for part in bases[:2]]
    high, low, own_arrival = prepare(
        row, owner // cuts, first_arrival.T, reflect_re[0], reflect_im[0], groups
    )
    if cuts > 1:
        size = half // cuts
        own_arrival = lax.dynamic_slice_in_dim(own_arrival, owner[0] % cuts * size, size, 1)

    field, adds = None, bases
    for section in range(ITERS):
        last = section == ITERS - 1
        sign = 1 if section % 2 == 0 else -1
        outs = product(row, field, adds, high, low, sign, points, groups, shards, last)
        if last:
            minus = outs[1:]
        copies = 1 if last else shards
        value = window(to_owners(outs[0]), own_arrival, points, copies)
        field = from_owners(value, "freq" if last else ("freq", "row"), copies)
        adds = bases if section % 2 == 1 else []
    plus = finish(field, *bases[:2])
    return tuple(part.T[None] for part in list(minus) + list(plus))


def solution(mesh):
    spec = P("freq", "row", None)
    return jax.shard_map(
        local,
        mesh=mesh,
        in_specs=(spec, spec, spec, spec, P("row", None)),
        out_specs=(spec, spec, spec, spec),
        check_vma=False,
    )
```

time: 159 us -> 139 us (0.87)
  blocking collectives: 73.5 us -> 115 us
  waiting for transfers between devices: 26.8 us -> 0.01 us
  local copies, waits for them, and re-layouts: 20 us -> 0.91 us
  starting transfers between devices: 14 us -> 3.14 us
  Pallas kernels: 23.2 us -> 19.2 us
    all_to_all x3 -> x4, blocking collectives: 36.3 us -> 60.4 us  [from_owners(): value = lax.all_to_all(value, axes, 0, 0, tiled=True)]
    all_to_all x3 -> x4, blocking collectives: 37.3 us -> 54.6 us  [to_owners(): return lax.all_to_all(value, 'freq', 0, 0, tiled=True)]
    all_to_all x2 -> x0, waiting for transfers between devices: 16.3 us -> none  [the longest x1 8.53 us: to_owners(): return lax.all_to_all(value, 'freq', 0, 0, tiled=True)]
    unnamed x32 -> x8, local copies, waits for them, and re-layouts: 13.6 us -> 0.91 us
    ppermute x4 -> x2, waiting for transfers between devices: 10.5 us -> 0.01 us  [shift(): lax.ppermute(value, 'row', [(i, (i - by) % shards) for i in range(shards)])]
    all_to_all x2 -> x0, starting transfers between devices: 9.47 us -> none  [the longest x1 5.95 us: to_owners(): return lax.all_to_all(value, 'freq', 0, 0, tiled=True)]
    another operation x7 -> x0, local copies, waits for them, and re-layouts: 5.8 us -> none  [the longest x4 2.9 us: out(): return [both[:, c].reshape(count, half).T[None] for c in range(2)]]
    pallas_call x13 -> x10, Pallas kernels: 23.2 us -> 19.2 us  [the longest x4 10.2 us: product(): pl.pallas_call(functools.partial(product_body, sign, points, shards, fiel...]
  transfers between devices with their start and end apart: 6 -> 2, of which waited for: 5 -> 0; matrix products, arithmetic and copies ran while one was open for 2% -> 0% of each run, Pallas kernels for 7% -> 4%
where the time goes in v1:
time: 139 us
  blocking collectives  115 us (83%)
  Pallas kernels  19.2 us (14%)
  starting transfers between devices  3.14 us (2%)
    all_to_all x4, blocking collectives, from_owners(): value = lax.all_to_all(value, axes, 0, 0, tiled=True)  60.4 us
    all_to_all x4, blocking collectives, to_owners(): return lax.all_to_all(value, 'freq', 0, 0, tiled=True)  54.6 us
    pallas_call x4, Pallas kernels, product(): pl.pallas_call(functools.partial(product_body, sign, points, shards, fiel...  10.2 us
    pallas_call x1, Pallas kernels, prepare(): pl.pallas_call(functools.partial(prepare_body, bands, groups), in_specs=[...  5.67 us
    ppermute x2, starting transfers between devices, shift(): lax.ppermute(value, 'row', [(i, (i - by) % shards) for i in range(shards)])  3.14 us
  transfers between devices with their start and end apart: 2, of which 0 were waited for; matrix products, arithmetic and copies ran while one was open for 0% of the time, Pallas kernels for 4%

profile of v1, /device:TPU:0, one launch (start us, length us, event | category | flops | bytes accessed | tf_op | source)
XLA Modules:
  0.0 139.0 jit_solution(4914249500204275408)
XLA Ops:
  0.6 3.1 %collective-permute-start = (f32[32,864]{1,0:T(8,128)}, f32[32,864]{1,0:T(8,128)S(1)}, u32[]{:S(2)}, u32[]{:S(2)}) collective-permute-start(f32[32,864]{1,0:T(8,128)} %bitcast.23), channel_id=1, source_target_pairs={{0,1},{1,0},{2,3},{3,2},{4,5},{5,4},{6,7},{7,6},{8,9},{9,8},{10,11... | collective-permute-start | bytes 331784 | tf_op jit(solution)/shard_map/ppermute | solution.py:301
  3.7 0.1 collective-permute-start.1
  3.8 0.0 copy-start.3
  3.8 0.9 copy-done.3
  4.7 0.0 copy-start.1
  4.7 0.0 copy-start.2
  4.7 5.7 %prepare.1 = (bf16[3456,864]{1,0:T(8,128)(2,1)S(1)}, bf16[3456,864]{1,0:T(8,128)(2,1)S(1)}, s32[4,864]{1,0:T(4,128)S(1)}) custom-call(s32[1]{0:T(128)} %bitcast.row_ref.refs_0_, s32[1]{0:T(128)} %bitcast.7.owner_ref, s32[32,864]{1,0:T(8,128)S(1)} %bitcast.31, f32[864,1728]{1,0:T(8,128)} %bitcast.32, f32[864,1728]{1,0:T(8,128)} %bitcast.33), custom_call_target="tpu_custom_call" | custom-call | flops 6115295232 | bytes 11943936 | tf_op jit(solution)/shard_map/prepare/pallas_call | solution.py:67
  10.3 0.0 collective-permute-done.refs_3_.refs_4_
  10.4 0.0 collective-permute-done.1.refs_4_.refs_5_
  10.4 0.0 copy-done.1
  10.4 0.0 copy-done.2
  10.4 0.0 copy-start
  10.4 2.5 %product.4 = f32[16,4,864]{2,1,0:T(4,128)S(1)} custom-call(s32[1]{0:T(128)} %bitcast.row_ref.refs_0_, f32[32,864]{1,0:T(8,128)S(1)} %bitcast.24, f32[32,864]{1,0:T(8,128)S(1)} %bitcast.28, f32[32,864]{1,0:T(8,128)S(1)} %collective-permute-done.refs_3_.refs_4_, f32[32,864]{1,0:T(8,128)S(1)} %collective-permute-done.1.refs_4_.refs_5_, ...), custom_call_target="tpu_custom_call" | custom-call | flops 1146617856 | bytes 11943936 | tf_op jit(solution)/shard_map/product/pallas_call | solution.py:152
  12.9 15.6 %all_to_all.40.g_ref = f32[16,4,864]{2,1,0:T(4,128)S(1)} all-to-all(f32[16,4,864]{2,1,0:T(4,128)S(1)} %product.4), channel_id=1, replica_groups=mesh['freq'=16,'row'=2] {'freq'}, dimensions={0} | all-to-all | bytes 442368 | tf_op jit(solution)/shard_map/all_to_all | solution.py:291
  28.5 0.0 copy-done
  28.5 0.6 window.4
  29.1 16.3 %all_to_all.41.refs_1_ = f32[32,4,864]{2,1,0:T(4,128)S(1)} all-to-all(f32[32,4,864]{2,1,0:T(4,128)S(1)} %window.4), channel_id=1, replica_groups=mesh['freq'=16,'row'=2] {'freq','row'}, dimensions={0} | all-to-all | bytes 884736 | tf_op jit(solution)/shard_map/all_to_all | solution.py:294
  45.4 2.3 %product.5 = f32[16,4,864]{2,1,0:T(4,128)S(1)} custom-call(s32[1]{0:T(128)} %bitcast.row_ref.refs_0_, f32[32,4,864]{2,1,0:T(4,128)S(1)} %all_to_all.41.refs_1_, bf16[3456,864]{1,0:T(8,128)(2,1)S(1)} %get-tuple-element.12.refs_5_.refs_2_.refs_6_, bf16[3456,864]{1,0:T(8,128)(2,1)S(1)} %get-tuple-element.13.refs_6_.refs_3_.refs_7_), custom_call_target="tpu_custom_call" | custom-call | flops 1146617856 | bytes 11943936 | tf_op jit(solution)/shard_map/product/pallas_call | solution.py:152
  47.7 13.0 %all_to_all.42.g_ref = f32[16,4,864]{2,1,0:T(4,128)S(1)} all-to-all(f32[16,4,864]{2,1,0:T(4,128)S(1)} %product.5), channel_id=1, replica_groups=mesh['freq'=16,'row'=2] {'freq'}, dimensions={0} | all-to-all | bytes 442368 | tf_op jit(solution)/shard_map/all_to_all | solution.py:291
  60.7 0.6 window.5
  61.3 16.0 %all_to_all.43.refs_1_ = f32[32,4,864]{2,1,0:T(4,128)S(1)} all-to-all(f32[32,4,864]{2,1,0:T(4,128)S(1)} %window.5), channel_id=1, replica_groups=mesh['freq'=16,'row'=2] {'freq','row'}, dimensions={0} | all-to-all | bytes 884736 | tf_op jit(solution)/shard_map/all_to_all | solution.py:294
  77.4 2.5 %product.6 = f32[16,4,864]{2,1,0:T(4,128)S(1)} custom-call(s32[1]{0:T(128)} %bitcast.row_ref.refs_0_, f32[32,4,864]{2,1,0:T(4,128)S(1)} %all_to_all.43.refs_1_, f32[32,864]{1,0:T(8,128)S(1)} %bitcast.25, f32[32,864]{1,0:T(8,128)S(1)} %bitcast.29, f32[32,864]{1,0:T(8,128)S(1)} %collective-permute-done.refs_3_.refs_4_, ...), custom_call_target="tpu_custom_call" | custom-call | flops 1146617856 | bytes 11943936 | tf_op jit(solution)/shard_map/product/pallas_call | solution.py:152
  79.8 13.0 %all_to_all.44.g_ref = f32[16,4,864]{2,1,0:T(4,128)S(1)} all-to-all(f32[16,4,864]{2,1,0:T(4,128)S(1)} %product.6), channel_id=1, replica_groups=mesh['freq'=16,'row'=2] {'freq'}, dimensions={0} | all-to-all | bytes 442368 | tf_op jit(solution)/shard_map/all_to_all | solution.py:291
  92.8 0.6 window.6
  93.5 16.0 %all_to_all.45.refs_1_ = f32[32,4,864]{2,1,0:T(4,128)S(1)} all-to-all(f32[32,4,864]{2,1,0:T(4,128)S(1)} %window.6), channel_id=1, replica_groups=mesh['freq'=16,'row'=2] {'freq','row'}, dimensions={0} | all-to-all | bytes 884736 | tf_op jit(solution)/shard_map/all_to_all | solution.py:294
  109.5 3.0 %product.7 = (f32[16,4,864]{2,1,0:T(4,128)S(1)}, f32[32,864]{1,0:T(8,128)}, f32[32,864]{1,0:T(8,128)}) custom-call(s32[1]{0:T(128)} %bitcast.row_ref.refs_0_, f32[32,4,864]{2,1,0:T(4,128)S(1)} %all_to_all.45.refs_1_, bf16[3456,864]{1,0:T(8,128)(2,1)S(1)} %get-tuple-element.12.refs_5_.refs_2_.refs_6_, ...), custom_call_target="tpu_custom_call" | custom-call | flops 1146617856 | bytes 11943936 | tf_op jit(solution)/shard_map/product/pallas_call | solution.py:152
  112.5 13.0 %all_to_all.46.g_ref = f32[16,4,864]{2,1,0:T(4,128)S(1)} all-to-all(f32[16,4,864]{2,1,0:T(4,128)S(1)} %get-tuple-element.17), channel_id=1, replica_groups=mesh['freq'=16,'row'=2] {'freq'}, dimensions={0} | all-to-all | bytes 442368 | tf_op jit(solution)/shard_map/all_to_all | solution.py:291
  125.5 0.6 window.7
  126.1 12.1 %all_to_all.47.value_ref = f32[16,4,864]{2,1,0:T(4,128)S(1)} all-to-all(f32[16,4,864]{2,1,0:T(4,128)S(1)} %window.7), channel_id=1, replica_groups=mesh['freq'=16,'row'=2] {'freq'}, dimensions={0} | all-to-all | bytes 442368 | tf_op jit(solution)/shard_map/all_to_all | solution.py:294
  138.2 0.8 finish.1
Async XLA Ops:
  0.6 9.7 %collective-permute-start = (f32[32,864]{1,0:T(8,128)}, f32[32,864]{1,0:T(8,128)S(1)}, u32[]{:S(2)}, u32[]{:S(2)}) collective-permute-start(f32[32,864]{1,0:T(8,128)} %bitcast.23), channel_id=1, source_target_pairs={{0,1},{1,0},{2,3},{3,2},{4,5},{5,4},{6,7},{7,6},{8,9},{9,8},{10,11... | collective-permute-start | bytes 331784 | tf_op jit(solution)/shard_map/ppermute | solution.py:301
  3.7 6.7 %collective-permute-start.1 = (f32[32,864]{1,0:T(8,128)}, f32[32,864]{1,0:T(8,128)S(1)}, u32[]{:S(2)}, u32[]{:S(2)}) collective-permute-start(f32[32,864]{1,0:T(8,128)} %bitcast.27), channel_id=1, source_target_pairs={{0,1},{1,0},{2,3},{3,2},{4,5},{5,4},{6,7},{7,6},{8,9},{9,8},{10,11... | collective-permute-start | bytes 331784 | tf_op jit(solution)/shard_map/ppermute | solution.py:301
  3.8 0.9 copy-start.3
  4.7 5.7 %copy-start.1 = (f32[1,864,32]{1,2,0:T(8,128)S(1)}, f32[1,864,32]{1,2,0:T(8,128)}, u32[]{:S(2)}) copy-start(f32[1,864,32]{1,2,0:T(8,128)} %param.11) | copy-start | bytes 331780
  4.7 5.7 %copy-start.2 = (f32[1,864,32]{1,2,0:T(8,128)S(1)}, f32[1,864,32]{1,2,0:T(8,128)}, u32[]{:S(2)}) copy-start(f32[1,864,32]{1,2,0:T(8,128)} %param.12) | copy-start | bytes 331780
  10.4 18.1 %copy-start = (f32[32,4,128]{2,1,0:T(4,128)S(1)}, f32[32,4,128]{2,1,0:T(4,128)}, u32[]{:S(2)}) copy-start(f32[32,4,128]{2,1,0:T(4,128)} %constant.25.clone.table_ref) | copy-start | bytes 196612

commit v2 on v1

--- a/solution.py
+++ b/solution.py
@@ -29,9 +29,18 @@
     return high, low
 
 
-def prepare_body(bands, groups, row_ref, owner_ref, arrival_ref, *refs):
-    re_ref, im_ref, high_ref, low_ref, own_ref, re_held, im_held, arrived = refs
-    full = re_ref.shape[1]
+def column_of(half, which, start):
+    main = half // LANES * LANES
+    return which * main + start if start < main else 2 * main + which * LANES
+
+
+def columns_in_all(half):
+    main = half // LANES * LANES
+    return 2 * main + (2 * LANES if main < half else 0)
+
+
+def prepare_body(bands, row_ref, owner_ref, re_ref, im_ref, high_ref, low_ref, re_held, im_held, arrived):
+    half, full = re_ref.shape
     pairs = ((re_ref, re_held), (im_ref, im_held))
     copies = {}
     for at, (start, size) in enumerate(bands):
@@ -41,34 +50,26 @@
                 source.at[rows], held.at[rows], arrived.at[at, which]
             )
             copies[at, which].start()
-    points = own_ref.shape[0] // 2
-    own = jnp.zeros(own_ref.shape, jnp.int32)
-    for g in range(groups):
-        mine = arrival_ref[g * points : (g + 1) * points]
-        own = jnp.where(owner_ref[0] == g, jnp.concatenate([mine, mine], axis=0), own)
-    own_ref[...] = own
     for at, (start, size) in enumerate(bands):
         for which, (_, held) in enumerate(pairs):
             copies[at, which].wait()
+            place = column_of(half, which, start)
             for column in range(0, full, LANES):
-                width = min(LANES, full - column)
-                piece = held[start : start + size, column : column + width]
-                high, low = split(piece.T)
-                rows = slice(which * full + column, which * full + column + width)
-                high_ref[rows, start : start + size] = high
-                low_ref[rows, start : start + size] = low
-
-
-def prepare(row, owner, arrival, reflect_re, reflect_im, groups):
+                rows = slice(column, min(column + LANES, full))
+                high, low = split(held[start : start + size, rows].T)
+                high_ref[rows, place : place + size] = high
+                low_ref[rows, place : place + size] = low
+
+
+def prepare(row, owner, reflect_re, reflect_im):
     half, full = reflect_re.shape
-    points = arrival.shape[0] // groups
     bands = [(start, min(LANES, half - start)) for start in range(0, half, LANES)]
-    shape = jax.ShapeDtypeStruct((2 * full, half), jnp.bfloat16)
+    shape = jax.ShapeDtypeStruct((full, columns_in_all(half)), jnp.bfloat16)
     return pl.pallas_call(
-        functools.partial(prepare_body, bands, groups),
-        in_specs=[whole(SMEM)] * 2 + [whole(VMEM)] + [whole(pltpu.HBM)] * 2,
-        out_specs=[whole(VMEM)] * 3,
-        out_shape=[shape] * 2 + [jax.ShapeDtypeStruct((2 * points, half), jnp.int32)],
+        functools.partial(prepare_body, bands),
+        in_specs=[whole(SMEM)] * 2 + [whole(pltpu.HBM)] * 2,
+        out_specs=[whole(VMEM)] * 2,
+        out_shape=[shape] * 2,
         scratch_shapes=[
             pltpu.VMEM((half, full), jnp.float32),
             pltpu.VMEM((half, full), jnp.float32),
@@ -79,19 +80,19 @@
             flops=32 * half * full * LANES, bytes_accessed=8 * half * full, transcendentals=0
         ),
         name="prepare",
-    )(row, owner, arrival, reflect_re, reflect_im)
-
-
-def product_body(sign, points, shards, joined, adds, emits, *refs):
+    )(row, owner, reflect_re, reflect_im)
+
+
+def product_body(sign, points, shards, joined, adds, first, *refs):
     refs = list(refs)
     row = refs.pop(0)[0]
     wide = refs.pop()
     field_ref = refs.pop(0) if joined else None
     bases = [refs.pop(0) for _ in range(2 * shards)] if adds else None
-    high_ref, low_ref, out_ref = refs[:3]
+    high_ref, low_ref = refs[:2]
+    out_ref = refs[4] if first else refs[2]
     groups, per, half = out_ref.shape
     rows = groups * per
-    full = shards * half
 
     def base(rows_in, place, part):
         chosen = bases[part][rows_in]
@@ -110,50 +111,49 @@
                 field = field_ref[g * shards + place]
                 value = field if value is None else field + value
             wide[g * per : (g + 1) * per, place * half : (place + 1) * half] = value
-    if emits:
+    if first:
+        owner_ref, arrival_ref, own_ref = refs[2], refs[3], refs[5]
+        own = jnp.zeros(own_ref.shape, jnp.int32)
         for g in range(groups):
-            value = field_ref[g * shards + row]
-            rows_out = slice(g * points, (g + 1) * points)
-            refs[3][rows_out] = value[:points]
-            refs[4][rows_out] = value[points:]
-    u = wide[...]
-    place = lax.broadcasted_iota(jnp.int32, u.shape, 0) % per
-    ahead = pltpu.roll(u, rows - points, 0)
-    behind = pltpu.roll(u, points, 0)
+            mine = arrival_ref[g * points : (g + 1) * points]
+            own = jnp.where(owner_ref[0] == g, jnp.concatenate([mine, mine], axis=0), own)
+        own_ref[...] = own
+    u_high, u_low = split(wide[...])
+    both = jnp.concatenate([u_high, u_low], axis=0)
+    one = jnp.dot(both, high_ref[...], preferred_element_type=jnp.float32)
+    two = jnp.dot(u_high, low_ref[...], preferred_element_type=jnp.float32)
+    result = one[:rows] + one[rows:] + two
+    main = half // LANES * LANES
+    parts = []
+    for which in range(2):
+        pieces = [result[:, which * main : (which + 1) * main]]
+        if main < half:
+            start = column_of(half, which, main)
+            pieces.append(result[:, start : start + half - main])
+        parts.append(jnp.concatenate(pieces, axis=1))
+    real, imaginary = parts
+    place = lax.broadcasted_iota(jnp.int32, imaginary.shape, 0) % per
+    ahead = pltpu.roll(imaginary, rows - points, 0)
+    behind = pltpu.roll(imaginary, points, 0)
     turned = jnp.where(place < points, -ahead, behind)
-    if sign < 0:
-        turned = -turned
-    u_high, u_low = split(u)
-    t_high, t_low = split(turned)
-
-    def times(left, ref, start):
-        return lax.dot_general(
-            left,
-            ref[start : start + full],
-            (((1,), (0,)), ((), ())),
-            preferred_element_type=jnp.float32,
-        )
-
-    one = times(jnp.concatenate([u_high, u_low], axis=0), high_ref, 0)
-    one = one + times(jnp.concatenate([t_high, t_low], axis=0), high_ref, full)
-    two = times(u_high, low_ref, 0) + times(t_high, low_ref, full)
-    result = one[:rows] + one[rows:] + two
+    total = real + turned if sign > 0 else real - turned
     for g in range(groups):
-        out_ref[g] = result[g * per : (g + 1) * per, :half]
-
-
-def product(row, field, bases, high, low, sign, points, groups, shards, emits):
-    half = high.shape[1]
+        out_ref[g] = total[g * per : (g + 1) * per]
+
+
+def product(row, field, bases, high, low, sign, points, groups, shards, half, extra):
     rows = 2 * points * groups
-    args = [row] + ([] if field is None else [field]) + bases + [high, low]
+    args = [row] + ([] if field is None else [field]) + bases + [high, low] + extra
+    spaces = [SMEM] + [VMEM] * (len(args) - 1)
     shapes = [jax.ShapeDtypeStruct((groups, 2 * points, half), jnp.float32)]
-    if emits:
-        shapes += [jax.ShapeDtypeStruct((groups * points, half), jnp.float32)] * 2
+    if extra:
+        spaces[-2] = SMEM
+        shapes.append(jax.ShapeDtypeStruct((2 * points, half), jnp.int32))
     return pl.pallas_call(
         functools.partial(
-            product_body, sign, points, shards, field is not None, bool(bases), emits
+            product_body, sign, points, shards, field is not None, bool(bases), bool(extra)
         ),
-        in_specs=[whole(SMEM)] + [whole(VMEM)] * (len(args) - 1),
+        in_specs=[whole(space) for space in spaces],
         out_specs=[whole(VMEM)] * len(shapes),
         out_shape=shapes,
         scratch_shapes=[pltpu.VMEM((rows, shards * half), jnp.float32)],
@@ -176,6 +176,7 @@
         ],
         axis=1,
     )
+    table = np.concatenate([table, table], axis=1)
     return np.repeat(table[:, :, None], LANES, 2).astype(np.float32)
 
 
@@ -185,20 +186,30 @@
 
 def window_body(freqs, points, copies, g_ref, arrival_ref, table_ref, out_ref):
     times = 2 * freqs
-    length = g_ref.shape[2]
+    per, length = g_ref.shape[1:]
     middle = times // 4
-    for start in range(0, length, LANES):
-        size = min(LANES, length - start)
-        lanes = slice(start, start + size)
-        arrival = arrival_ref[:, lanes]
+    tiles = [slice(start, min(start + LANES, length)) for start in range(0, length, LANES)]
+    stacks = [tiles[i : i + 2] for i in range(0, len(tiles) - 1, 2)]
+    if sum(len(stack) for stack in stacks) < len(tiles):
+        stacks.append(tiles[-1:])
+    if len(stacks[-1]) == 2 and length % LANES:
+        stacks[-1:] = [stacks[-1][:1], stacks[-1][1:]]
+    for stack in stacks:
+        size = stack[0].stop - stack[0].start
+        height = per * len(stack)
+
+        def stacked(read):
+            pieces = [read(lanes) for lanes in stack]
+            return pieces[0] if len(pieces) == 1 else jnp.concatenate(pieces, axis=0)
 
         def tab(t, k):
-            return table_ref[t * k % times][:, :size]
-
+            return table_ref[t * k % times][:height, :size]
+
+        arrival = stacked(lambda lanes: arrival_ref[:, lanes])
         g = []
         for k in range(freqs):
             weight = (1.0 if k == 0 else 2.0) / times
-            g.append(g_ref[k][:, lanes] * weight)
+            g.append(stacked(lambda lanes: g_ref[k][:, lanes]) * weight)
         plus, minus = [], []
         for t in range(middle + 1):
             even = add_all([tab(t, k) * g[k] for k in range(0, freqs, 2)])
@@ -215,8 +226,9 @@
         for k in range(freqs):
             source = plus if k % 2 == 0 else minus
             value = add_all([tab(t, k) * source[t] for t in range(middle + 1)])
-            for copy in range(copies):
-                out_ref[k * copies + copy, :, lanes] = value
+            for at, lanes in enumerate(stack):
+                for copy in range(copies):
+                    out_ref[k * copies + copy, :, lanes] = value[at * per : (at + 1) * per]
 
 
 def window_small(g, arrival, points, copies):
@@ -254,24 +266,31 @@
     return jnp.repeat(jnp.concatenate(outs, axis=1), copies, axis=0)
 
 
-def finish_body(points, value_ref, base_re_ref, base_im_ref, re_ref, im_ref):
-    for g in range(value_ref.shape[0]):
-        value = value_ref[g]
+def finish_body(points, shards, row_ref, minus_ref, update_ref, *refs):
+    base_re_ref, base_im_ref, minus_re_ref, minus_im_ref, plus_re_ref, plus_im_ref = refs
+    row = row_ref[0]
+    for g in range(update_ref.shape[0]):
         rows = slice(g * points, (g + 1) * points)
-        re_ref[rows] = value[:points] + base_re_ref[rows]
-        im_ref[rows] = value[points:] + base_im_ref[rows]
-
-
-def finish(value, base_re, base_im):
-    points = value.shape[1] // 2
+        value = minus_ref[g * shards]
+        for place in range(1, shards):
+            value = jnp.where(row == place, minus_ref[g * shards + place], value)
+        minus_re_ref[rows] = value[:points]
+        minus_im_ref[rows] = value[points:]
+        value = update_ref[g]
+        plus_re_ref[rows] = value[:points] + base_re_ref[rows]
+        plus_im_ref[rows] = value[points:] + base_im_ref[rows]
+
+
+def finish(row, minus, update, base_re, base_im, shards):
+    points = update.shape[1] // 2
     return pl.pallas_call(
-        functools.partial(finish_body, points),
-        in_specs=[whole(VMEM)] * 3,
-        out_specs=[whole(VMEM)] * 2,
-        out_shape=[jax.ShapeDtypeStruct(base_re.shape, jnp.float32)] * 2,
+        functools.partial(finish_body, points, shards),
+        in_specs=[whole(SMEM)] + [whole(VMEM)] * 4,
+        out_specs=[whole(VMEM)] * 4,
+        out_shape=[jax.ShapeDtypeStruct(base_re.shape, jnp.float32)] * 4,
         compiler_params=pltpu.CompilerParams(vmem_limit_bytes=8 << 20),
         name="finish",
-    )(value, base_re, base_im)
+    )(row, minus, update, base_re, base_im)
 
 
 def local(reflect_re, reflect_im, focus_re, focus_im, first_arrival):
@@ -282,7 +301,7 @@
     points = count // groups
     cuts = owners // groups
     row = lax.axis_index("row").reshape(1)
-    owner = lax.axis_index("freq").reshape(1)
+    owner = (lax.axis_index("freq") // cuts).reshape(1)
 
     def to_owners(value):
         if cuts > 1:
@@ -304,26 +323,27 @@
     bases = [focus_re[0].T, focus_im[0].T]
     for by in range(1, shards):
         bases += [shift(part, by) for part in bases[:2]]
-    high, low, own_arrival = prepare(
-        row, owner // cuts, first_arrival.T, reflect_re[0], reflect_im[0], groups
-    )
-    if cuts > 1:
-        size = half // cuts
-        own_arrival = lax.dynamic_slice_in_dim(own_arrival, owner[0] % cuts * size, size, 1)
-
-    field, adds = None, bases
+    high, low = prepare(row, owner, reflect_re[0], reflect_im[0])
+
+    field, adds, extra = None, bases, [owner, first_arrival.T]
     for section in range(ITERS):
         last = section == ITERS - 1
         sign = 1 if section % 2 == 0 else -1
-        outs = product(row, field, adds, high, low, sign, points, groups, shards, last)
-        if last:
-            minus = outs[1:]
+        outs = product(row, field, adds, high, low, sign, points, groups, shards, half, extra)
+        if extra:
+            own_arrival, extra = outs[1], []
+            if cuts > 1:
+                size = half // cuts
+                start = lax.axis_index("freq") % cuts * size
+                own_arrival = lax.dynamic_slice_in_dim(own_arrival, start, size, 1)
         copies = 1 if last else shards
         value = window(to_owners(outs[0]), own_arrival, points, copies)
+        if last:
+            minus = field
         field = from_owners(value, "freq" if last else ("freq", "row"), copies)
         adds = bases if section % 2 == 1 else []
-    plus = finish(field, *bases[:2])
-    return tuple(part.T[None] for part in list(minus) + list(plus))
+    results = finish(row, minus, field, *bases[:2], shards)
+    return tuple(part.T[None] for part in results)
 
 
 def solution(mesh):

time: 139 us -> 136 us (0.978)
  Pallas kernels: 19.2 us -> 17.2 us
where the time goes in v2:
time: 136 us
  blocking collectives  115 us (85%)
  Pallas kernels  17.2 us (13%)
  starting transfers between devices  3.14 us (2%)
    all_to_all x4, blocking collectives, from_owners(): value = lax.all_to_all(value, axes, 0, 0, tiled=True)  60.4 us
    all_to_all x4, blocking collectives, to_owners(): return lax.all_to_all(value, 'freq', 0, 0, tiled=True)  54.6 us
    pallas_call x4, Pallas kernels, product(): pl.pallas_call(functools.partial(product_body, sign, points, shards, fiel...  8.99 us
    pallas_call x1, Pallas kernels, prepare(): pl.pallas_call(functools.partial(prepare_body, bands), in_specs=[whole(SM...  5.67 us
    ppermute x2, starting transfers between devices, shift(): lax.ppermute(value, 'row', [(i, (i - by) % shards) for i in range(shards)])  3.14 us
  transfers between devices with their start and end apart: 2, of which 0 were waited for; matrix products, arithmetic and copies ran while one was open for 0% of the time, Pallas kernels for 4%

profile of v2, /device:TPU:0, one launch (start us, length us, event | category | flops | bytes accessed | tf_op | source)
XLA Modules:
  0.0 136.1 jit_solution(12941318125776379718)
XLA Ops:
  0.6 3.1 %collective-permute-start = (f32[32,864]{1,0:T(8,128)}, f32[32,864]{1,0:T(8,128)S(1)}, u32[]{:S(2)}, u32[]{:S(2)}) collective-permute-start(f32[32,864]{1,0:T(8,128)} %bitcast.23), channel_id=1, source_target_pairs={{0,1},{1,0},{2,3},{3,2},{4,5},{5,4},{6,7},{7,6},{8,9},{9,8},{10,11... | collective-permute-start | bytes 331784 | tf_op jit(solution)/shard_map/ppermute | solution.py:320
  3.7 0.1 collective-permute-start.1
  3.8 0.0 copy-start.1
  3.8 0.0 copy-start.2
  3.8 0.0 copy-start.3
  3.8 5.7 %prepare.1 = (bf16[1728,1792]{1,0:T(8,128)(2,1)S(1)}, bf16[1728,1792]{1,0:T(8,128)(2,1)S(1)}) custom-call(s32[1]{0:T(128)} %bitcast.row_ref.refs_0_, s32[1]{0:T(128)} %bitcast.7.owner_ref.refs_7_, f32[864,1728]{1,0:T(8,128)} %bitcast.32, f32[864,1728]{1,0:T(8,128)} %bitcast.33), custom_call_target="tpu_custom_call" | custom-call | flops 6115295232 | bytes 11943936 | tf_op jit(solution)/shard_map/prepare/pallas_call | solution.py:68
  9.5 0.0 collective-permute-done.refs_3_.refs_4_
  9.5 0.0 collective-permute-done.1.refs_4_.refs_5_
  9.5 0.0 copy-done.1
  9.5 0.0 copy-done.2
  9.5 0.0 copy-done.3
  9.5 0.0 copy-start
  9.5 2.4 %product.4 = (f32[16,4,864]{2,1,0:T(4,128)S(1)}, s32[4,864]{1,0:T(4,128)S(1)}) custom-call(s32[1]{0:T(128)} %bitcast.row_ref.refs_0_, f32[32,864]{1,0:T(8,128)S(1)} %bitcast.24, f32[32,864]{1,0:T(8,128)S(1)} %bitcast.28, f32[32,864]{1,0:T(8,128)S(1)} %collective-permute-done.refs_3_.refs_4_, f32[32,864]{1,0:T(8,128)S(1)} %collective-permute-done.1.refs_4_.refs_5_, ...), custom_call_target="tpu_custom_call" | custom-call | flops 1146617856 | bytes 11943936 | tf_op jit(solution)/shard_map/product/pallas_call | solution.py:152
  11.9 15.6 %all_to_all.40.g_ref = f32[16,4,864]{2,1,0:T(4,128)S(1)} all-to-all(f32[16,4,864]{2,1,0:T(4,128)S(1)} %get-tuple-element.14), channel_id=1, replica_groups=mesh['freq'=16,'row'=2] {'freq'}, dimensions={0} | all-to-all | bytes 442368 | tf_op jit(solution)/shard_map/all_to_all | solution.py:310
  27.5 0.0 copy-done
  27.5 0.4 window.4
  27.9 16.3 %all_to_all.41.refs_1_ = f32[32,4,864]{2,1,0:T(4,128)S(1)} all-to-all(f32[32,4,864]{2,1,0:T(4,128)S(1)} %window.4), channel_id=1, replica_groups=mesh['freq'=16,'row'=2] {'freq','row'}, dimensions={0} | all-to-all | bytes 884736 | tf_op jit(solution)/shard_map/all_to_all | solution.py:313
  44.2 2.1 %product.5 = f32[16,4,864]{2,1,0:T(4,128)S(1)} custom-call(s32[1]{0:T(128)} %bitcast.row_ref.refs_0_, f32[32,4,864]{2,1,0:T(4,128)S(1)} %all_to_all.41.refs_1_, bf16[1728,1792]{1,0:T(8,128)(2,1)S(1)} %get-tuple-element.12.refs_5_.refs_2_.refs_6_, bf16[1728,1792]{1,0:T(8,128)(2,1)S(1)} %get-tuple-element.13.refs_6_.refs_3_.refs_7_), custom_call_target="tpu_custom_call" | custom-call | flops 1146617856 | bytes 11943936 | tf_op jit(solution)/shard_map/product/pallas_call | solution.py:152
  46.3 13.0 %all_to_all.42.g_ref = f32[16,4,864]{2,1,0:T(4,128)S(1)} all-to-all(f32[16,4,864]{2,1,0:T(4,128)S(1)} %product.5), channel_id=1, replica_groups=mesh['freq'=16,'row'=2] {'freq'}, dimensions={0} | all-to-all | bytes 442368 | tf_op jit(solution)/shard_map/all_to_all | solution.py:310
  59.3 0.4 window.5
  59.7 16.0 %all_to_all.43.refs_1_ = f32[32,4,864]{2,1,0:T(4,128)S(1)} all-to-all(f32[32,4,864]{2,1,0:T(4,128)S(1)} %window.5), channel_id=1, replica_groups=mesh['freq'=16,'row'=2] {'freq','row'}, dimensions={0} | all-to-all | bytes 884736 | tf_op jit(solution)/shard_map/all_to_all | solution.py:313
  75.8 2.3 %product.6 = f32[16,4,864]{2,1,0:T(4,128)S(1)} custom-call(s32[1]{0:T(128)} %bitcast.row_ref.refs_0_, f32[32,4,864]{2,1,0:T(4,128)S(1)} %all_to_all.43.refs_1_, f32[32,864]{1,0:T(8,128)S(1)} %bitcast.25, f32[32,864]{1,0:T(8,128)S(1)} %bitcast.29, f32[32,864]{1,0:T(8,128)S(1)} %collective-permute-done.refs_3_.refs_4_, ...), custom_call_target="tpu_custom_call" | custom-call | flops 1146617856 | bytes 11943936 | tf_op jit(solution)/shard_map/product/pallas_call | solution.py:152
  78.1 13.0 %all_to_all.44.g_ref = f32[16,4,864]{2,1,0:T(4,128)S(1)} all-to-all(f32[16,4,864]{2,1,0:T(4,128)S(1)} %product.6), channel_id=1, replica_groups=mesh['freq'=16,'row'=2] {'freq'}, dimensions={0} | all-to-all | bytes 442368 | tf_op jit(solution)/shard_map/all_to_all | solution.py:310
  91.1 0.4 window.6
  91.5 16.0 %all_to_all.45.refs_1_.minus_ref = f32[32,4,864]{2,1,0:T(4,128)S(1)} all-to-all(f32[32,4,864]{2,1,0:T(4,128)S(1)} %window.6), channel_id=1, replica_groups=mesh['freq'=16,'row'=2] {'freq','row'}, dimensions={0} | all-to-all | bytes 884736 | tf_op jit(solution)/shard_map/all_to_all | solution.py:313
  107.5 2.1 %product.7 = f32[16,4,864]{2,1,0:T(4,128)S(1)} custom-call(s32[1]{0:T(128)} %bitcast.row_ref.refs_0_, f32[32,4,864]{2,1,0:T(4,128)S(1)} %all_to_all.45.refs_1_.minus_ref, bf16[1728,1792]{1,0:T(8,128)(2,1)S(1)} %get-tuple-element.12.refs_5_.refs_2_.refs_6_, bf16[1728,1792]{1,0:T(8,128)(2,1)S(1)} %get-tuple-element.13.refs_6_.refs_3_.refs_7_), custom_call_target="tpu_custom_call" | custom-call | flops 1146617856 | bytes 11943936 | tf_op jit(solution)/shard_map/product/pallas_call | solution.py:152
  109.7 13.0 %all_to_all.46.g_ref = f32[16,4,864]{2,1,0:T(4,128)S(1)} all-to-all(f32[16,4,864]{2,1,0:T(4,128)S(1)} %product.7), channel_id=1, replica_groups=mesh['freq'=16,'row'=2] {'freq'}, dimensions={0} | all-to-all | bytes 442368 | tf_op jit(solution)/shard_map/all_to_all | solution.py:310
  122.7 0.4 window.7
  123.1 12.1 %all_to_all.47.update_ref = f32[16,4,864]{2,1,0:T(4,128)S(1)} all-to-all(f32[16,4,864]{2,1,0:T(4,128)S(1)} %window.7), channel_id=1, replica_groups=mesh['freq'=16,'row'=2] {'freq'}, dimensions={0} | all-to-all | bytes 442368 | tf_op jit(solution)/shard_map/all_to_all | solution.py:313
  135.1 0.9 finish.1
Async XLA Ops:
  0.6 8.8 %collective-permute-start = (f32[32,864]{1,0:T(8,128)}, f32[32,864]{1,0:T(8,128)S(1)}, u32[]{:S(2)}, u32[]{:S(2)}) collective-permute-start(f32[32,864]{1,0:T(8,128)} %bitcast.23), channel_id=1, source_target_pairs={{0,1},{1,0},{2,3},{3,2},{4,5},{5,4},{6,7},{7,6},{8,9},{9,8},{10,11... | collective-permute-start | bytes 331784 | tf_op jit(solution)/shard_map/ppermute | solution.py:320
  3.7 5.8 %collective-permute-start.1 = (f32[32,864]{1,0:T(8,128)}, f32[32,864]{1,0:T(8,128)S(1)}, u32[]{:S(2)}, u32[]{:S(2)}) collective-permute-start(f32[32,864]{1,0:T(8,128)} %bitcast.27), channel_id=1, source_target_pairs={{0,1},{1,0},{2,3},{3,2},{4,5},{5,4},{6,7},{7,6},{8,9},{9,8},{10,11... | collective-permute-start | bytes 331784 | tf_op jit(solution)/shard_map/ppermute | solution.py:320
  3.8 5.7 %copy-start.1 = (f32[1,864,32]{1,2,0:T(8,128)S(1)}, f32[1,864,32]{1,2,0:T(8,128)}, u32[]{:S(2)}) copy-start(f32[1,864,32]{1,2,0:T(8,128)} %param.11) | copy-start | bytes 331780
  3.8 5.7 %copy-start.2 = (f32[1,864,32]{1,2,0:T(8,128)S(1)}, f32[1,864,32]{1,2,0:T(8,128)}, u32[]{:S(2)}) copy-start(f32[1,864,32]{1,2,0:T(8,128)} %param.12) | copy-start | bytes 331780
  3.8 5.7 %copy-start.3 = (s32[864,32]{0,1:T(8,128)S(1)}, s32[864,32]{0,1:T(8,128)}, u32[]{:S(2)}) copy-start(s32[864,32]{0,1:T(8,128)} %param.13) | copy-start | bytes 331780
  9.5 18.0 %copy-start = (f32[32,8,128]{2,1,0:T(8,128)S(1)}, f32[32,8,128]{2,1,0:T(8,128)}, u32[]{:S(2)}) copy-start(f32[32,8,128]{2,1,0:T(8,128)} %constant.21.clone.table_ref) | copy-start | bytes 393220

commit v3 on v2

--- a/solution.py
+++ b/solution.py
@@ -13,6 +13,7 @@
 VMEM = pltpu.VMEM
 SMEM = pltpu.SMEM
 LANES = 128
+TILE = 256
 
 
 def up(value, unit):
@@ -29,17 +30,18 @@
     return high, low
 
 
-def column_of(half, which, start):
-    main = half // LANES * LANES
-    return which * main + start if start < main else 2 * main + which * LANES
-
-
-def columns_in_all(half):
-    main = half // LANES * LANES
-    return 2 * main + (2 * LANES if main < half else 0)
-
-
-def prepare_body(bands, row_ref, owner_ref, re_ref, im_ref, high_ref, low_ref, re_held, im_held, arrived):
+def pieces_of(half):
+    return [(start, min(TILE, half - start)) for start in range(0, half, TILE)]
+
+
+def columns_of(half):
+    whole_pieces = half // TILE * 2 * TILE
+    rest = 4 * up(half % TILE, LANES)
+    return [whole_pieces] * 2 + ([rest] if rest else [])
+
+
+def prepare_body(bands, row_ref, owner_ref, re_ref, im_ref, *refs):
+    *outs, re_held, im_held, arrived = refs
     half, full = re_ref.shape
     pairs = ((re_ref, re_held), (im_ref, im_held))
     copies = {}
@@ -53,23 +55,30 @@
     for at, (start, size) in enumerate(bands):
         for which, (_, held) in enumerate(pairs):
             copies[at, which].wait()
-            place = column_of(half, which, start)
-            for column in range(0, full, LANES):
-                rows = slice(column, min(column + LANES, full))
-                high, low = split(held[start : start + size, rows].T)
-                high_ref[rows, place : place + size] = high
-                low_ref[rows, place : place + size] = low
+            first = start // TILE * TILE
+            if first + TILE <= half:
+                place = 2 * first + which * TILE + start - first
+                targets = [(outs[0], place), (outs[1], place)]
+            else:
+                width = up(half - first, LANES)
+                place = which * width + start - first
+                targets = [(outs[2], place), (outs[2], place + 2 * width)]
+            for line in range(0, full, LANES):
+                rows = slice(line, min(line + LANES, full))
+                parts = split(held[start : start + size, rows].T)
+                for (target, place), part in zip(targets, parts):
+                    target[rows, place : place + size] = part
 
 
 def prepare(row, owner, reflect_re, reflect_im):
     half, full = reflect_re.shape
     bands = [(start, min(LANES, half - start)) for start in range(0, half, LANES)]
-    shape = jax.ShapeDtypeStruct((full, columns_in_all(half)), jnp.bfloat16)
+    shapes = [jax.ShapeDtypeStruct((full, width), jnp.bfloat16) for width in columns_of(half)]
     return pl.pallas_call(
         functools.partial(prepare_body, bands),
         in_specs=[whole(SMEM)] * 2 + [whole(pltpu.HBM)] * 2,
-        out_specs=[whole(VMEM)] * 2,
-        out_shape=[shape] * 2,
+        out_specs=[whole(VMEM)] * len(shapes),
+        out_shape=shapes,
         scratch_shapes=[
             pltpu.VMEM((half, full), jnp.float32),
             pltpu.VMEM((half, full), jnp.float32),
@@ -83,80 +92,80 @@
     )(row, owner, reflect_re, reflect_im)
 
 
-def product_body(sign, points, shards, joined, adds, first, *refs):
+def product_body(sign, points, shards, first, adds, *refs):
     refs = list(refs)
-    row = refs.pop(0)[0]
-    wide = refs.pop()
-    field_ref = refs.pop(0) if joined else None
-    bases = [refs.pop(0) for _ in range(2 * shards)] if adds else None
-    high_ref, low_ref = refs[:2]
-    out_ref = refs[4] if first else refs[2]
+    if first:
+        row_ref, owner_ref, arrival_ref = refs[:3]
+        bases, refs = refs[3 : 3 + 2 * shards], refs[3 + 2 * shards :]
+        *weights, out_ref, own_ref, wide = refs
+    else:
+        field_ref = refs.pop(0)
+        base_ref = refs.pop(0) if adds else None
+        *weights, out_ref, wide = refs
     groups, per, half = out_ref.shape
     rows = groups * per
-
-    def base(rows_in, place, part):
-        chosen = bases[part][rows_in]
-        for by in range(1, shards):
-            here = (row + by) % shards == place
-            chosen = jnp.where(here, bases[2 * by + part][rows_in], chosen)
-        return chosen
-
-    for g in range(groups):
-        rows_in = slice(g * points, (g + 1) * points)
-        for place in range(shards):
-            value = None
-            if adds:
-                value = jnp.concatenate([base(rows_in, place, part) for part in range(2)], axis=0)
-            if joined:
-                field = field_ref[g * shards + place]
-                value = field if value is None else field + value
-            wide[g * per : (g + 1) * per, place * half : (place + 1) * half] = value
     if first:
-        owner_ref, arrival_ref, own_ref = refs[2], refs[3], refs[5]
+        for row in range(shards):
+
+            @pl.when(row_ref[0] == row)
+            def _():
+                for g in range(groups):
+                    for by in range(shards):
+                        start = (row + by) % shards * half
+                        for part in range(2):
+                            target = g * per + part * points
+                            wide[target : target + points, start : start + half] = bases[
+                                2 * by + part
+                            ][g * points : (g + 1) * points]
+
         own = jnp.zeros(own_ref.shape, jnp.int32)
         for g in range(groups):
             mine = arrival_ref[g * points : (g + 1) * points]
             own = jnp.where(owner_ref[0] == g, jnp.concatenate([mine, mine], axis=0), own)
         own_ref[...] = own
-    u_high, u_low = split(wide[...])
+    else:
+        for g in range(groups):
+            band = slice(g * per, (g + 1) * per)
+            for place in range(shards):
+                lanes = slice(place * half, (place + 1) * half)
+                wide[band, lanes] = field_ref[g * shards + place]
+    u = wide[...] + base_ref[...] if adds else wide[...]
+    u_high, u_low = split(u)
     both = jnp.concatenate([u_high, u_low], axis=0)
-    one = jnp.dot(both, high_ref[...], preferred_element_type=jnp.float32)
-    two = jnp.dot(u_high, low_ref[...], preferred_element_type=jnp.float32)
-    result = one[:rows] + one[rows:] + two
-    main = half // LANES * LANES
-    parts = []
-    for which in range(2):
-        pieces = [result[:, which * main : (which + 1) * main]]
-        if main < half:
-            start = column_of(half, which, main)
-            pieces.append(result[:, start : start + half - main])
-        parts.append(jnp.concatenate(pieces, axis=1))
-    real, imaginary = parts
-    place = lax.broadcasted_iota(jnp.int32, imaginary.shape, 0) % per
-    ahead = pltpu.roll(imaginary, rows - points, 0)
-    behind = pltpu.roll(imaginary, points, 0)
-    turned = jnp.where(place < points, -ahead, behind)
-    total = real + turned if sign > 0 else real - turned
-    for g in range(groups):
-        out_ref[g] = total[g * per : (g + 1) * per]
-
-
-def product(row, field, bases, high, low, sign, points, groups, shards, half, extra):
+    for start, size in pieces_of(half):
+        width = up(size, LANES)
+        if size == TILE:
+            columns = slice(2 * start, 2 * start + 2 * TILE)
+            one = jnp.dot(both, weights[0][:, columns], preferred_element_type=jnp.float32)
+            two = jnp.dot(u_high, weights[1][:, columns], preferred_element_type=jnp.float32)
+        else:
+            one = jnp.dot(both, weights[2][...], preferred_element_type=jnp.float32)
+            one, two = one[:, : 2 * width], one[:rows, 2 * width :]
+        result = one[:rows] + one[rows:] + two
+        real, imaginary = result[:, :size], result[:, width : width + size]
+        place = lax.broadcasted_iota(jnp.int32, imaginary.shape, 0) % per
+        ahead = pltpu.roll(imaginary, rows - points, 0)
+        behind = pltpu.roll(imaginary, points, 0)
+        turned = jnp.where(place < points, -ahead, behind)
+        total = real + turned if sign > 0 else real - turned
+        for g in range(groups):
+            out_ref[g, :, start : start + size] = total[g * per : (g + 1) * per]
+
+
+def product(before, base, after, sign, points, groups, shards, half):
+    first = len(before) > 1
     rows = 2 * points * groups
-    args = [row] + ([] if field is None else [field]) + bases + [high, low] + extra
-    spaces = [SMEM] + [VMEM] * (len(args) - 1)
+    args = before + ([] if base is None else [base]) + after
+    field = jax.ShapeDtypeStruct((rows, shards * half), jnp.float32)
     shapes = [jax.ShapeDtypeStruct((groups, 2 * points, half), jnp.float32)]
-    if extra:
-        spaces[-2] = SMEM
-        shapes.append(jax.ShapeDtypeStruct((2 * points, half), jnp.int32))
+    if first:
+        shapes += [jax.ShapeDtypeStruct((2 * points, half), jnp.int32), field]
     return pl.pallas_call(
-        functools.partial(
-            product_body, sign, points, shards, field is not None, bool(bases), bool(extra)
-        ),
-        in_specs=[whole(space) for space in spaces],
+        functools.partial(product_body, sign, points, shards, first, base is not None),
+        in_specs=[whole(SMEM if first and at < 2 else VMEM) for at in range(len(args))],
         out_specs=[whole(VMEM)] * len(shapes),
         out_shape=shapes,
-        scratch_shapes=[pltpu.VMEM((rows, shards * half), jnp.float32)],
+        scratch_shapes=[] if first else [pltpu.VMEM(field.shape, jnp.float32)],
         compiler_params=pltpu.CompilerParams(vmem_limit_bytes=24 << 20),
         cost_estimate=pl.CostEstimate(
             flops=12 * rows * shards * half * half,
@@ -283,11 +292,12 @@
 
 def finish(row, minus, update, base_re, base_im, shards):
     points = update.shape[1] // 2
+    shape = jax.ShapeDtypeStruct(base_re.shape, jnp.float32)
     return pl.pallas_call(
         functools.partial(finish_body, points, shards),
         in_specs=[whole(SMEM)] + [whole(VMEM)] * 4,
         out_specs=[whole(VMEM)] * 4,
-        out_shape=[jax.ShapeDtypeStruct(base_re.shape, jnp.float32)] * 4,
+        out_shape=[shape] * 4,
         compiler_params=pltpu.CompilerParams(vmem_limit_bytes=8 << 20),
         name="finish",
     )(row, minus, update, base_re, base_im)
@@ -323,15 +333,15 @@
     bases = [focus_re[0].T, focus_im[0].T]
     for by in range(1, shards):
         bases += [shift(part, by) for part in bases[:2]]
-    high, low = prepare(row, owner, reflect_re[0], reflect_im[0])
-
-    field, adds, extra = None, bases, [owner, first_arrival.T]
+    weights = list(prepare(row, owner, reflect_re[0], reflect_im[0]))
+
+    before, adds = [row, owner, first_arrival.T] + bases, None
     for section in range(ITERS):
         last = section == ITERS - 1
         sign = 1 if section % 2 == 0 else -1
-        outs = product(row, field, adds, high, low, sign, points, groups, shards, half, extra)
-        if extra:
-            own_arrival, extra = outs[1], []
+        outs = product(before, adds, weights, sign, points, groups, shards, half)
+        if section == 0:
+            own_arrival, whole_base = outs[1:]
             if cuts > 1:
                 size = half // cuts
                 start = lax.axis_index("freq") % cuts * size
@@ -339,10 +349,10 @@
         copies = 1 if last else shards
         value = window(to_owners(outs[0]), own_arrival, points, copies)
         if last:
-            minus = field
-        field = from_owners(value, "freq" if last else ("freq", "row"), copies)
-        adds = bases if section % 2 == 1 else []
-    results = finish(row, minus, field, *bases[:2], shards)
+            minus = before[0]
+        before = [from_owners(value, "freq" if last else ("freq", "row"), copies)]
+        adds = whole_base if section % 2 == 1 else None
+    results = finish(row, minus, before[0], *bases[:2], shards)
     return tuple(part.T[None] for part in results)
 
 

time: 136 us -> 136 us (level)
  no operation moved by 1% of the time
where the time goes in v3:
time: 136 us; the launch traced here: 135 us
  blocking collectives  115 us (85%)
  Pallas kernels  16.4 us (12%)
  starting transfers between devices  3.14 us (2%)
    all_to_all x4, blocking collectives, from_owners(): value = lax.all_to_all(value, axes, 0, 0, tiled=True)  60.4 us
    all_to_all x4, blocking collectives, to_owners(): return lax.all_to_all(value, 'freq', 0, 0, tiled=True)  54.7 us
    pallas_call x4, Pallas kernels, product(): pl.pallas_call(functools.partial(product_body, sign, points, shards, firs...  8.21 us
    pallas_call x1, Pallas kernels, prepare(): pl.pallas_call(functools.partial(prepare_body, bands), in_specs=[whole(SM...  5.67 us
    ppermute x2, starting transfers between devices, shift(): lax.ppermute(value, 'row', [(i, (i - by) % shards) for i in range(shards)])  3.14 us
  transfers between devices with their start and end apart: 2, of which 0 were waited for; matrix products, arithmetic and copies ran while one was open for 0% of the time, Pallas kernels for 4%

profile of v3, /device:TPU:0, one launch (start us, length us, event | category | flops | bytes accessed | tf_op | source)
XLA Modules:
  0.0 135.3 jit_solution(8671599307976280703)
XLA Ops:
  0.6 3.1 %collective-permute-start = (f32[32,864]{1,0:T(8,128)}, f32[32,864]{1,0:T(8,128)S(1)}, u32[]{:S(2)}, u32[]{:S(2)}) collective-permute-start(f32[32,864]{1,0:T(8,128)} %bitcast.23), channel_id=1, source_target_pairs={{0,1},{1,0},{2,3},{3,2},{4,5},{5,4},{6,7},{7,6},{8,9},{9,8},{10,11... | collective-permute-start | bytes 331784 | tf_op jit(solution)/shard_map/ppermute | solution.py:330
  3.7 0.1 collective-permute-start.1
  3.8 0.0 copy-start.1
  3.8 0.0 copy-start.2
  3.8 0.0 copy-start.3
  3.8 5.7 %prepare.1 = (bf16[1728,1536]{1,0:T(8,128)(2,1)S(1)}, bf16[1728,1536]{1,0:T(8,128)(2,1)S(1)}, bf16[1728,512]{1,0:T(8,128)(2,1)S(1)}) custom-call(s32[1]{0:T(128)} %bitcast.row_ref.refs_0_, s32[1]{0:T(128)} %bitcast.1.owner_ref.refs_1_, f32[864,1728]{1,0:T(8,128)} %bitcast.30, f32[864,1728]{1,0:T(8,128)} %bitcast.31), custom_call_target="tpu_custom_call" | custom-call | flops 6115295232 | bytes 11943936 | tf_op jit(solution)/shard_map/prepare/pallas_call | solution.py:77
  9.5 0.0 collective-permute-done.refs_5_
  9.5 0.0 collective-permute-done.1.refs_6_
  9.5 0.0 copy-done.1
  9.5 0.0 copy-done.2
  9.5 0.0 copy-done.3
  9.5 0.0 copy-start
  9.5 2.2 %product.4 = (f32[16,4,864]{2,1,0:T(4,128)S(1)}, s32[4,864]{1,0:T(4,128)S(1)}, f32[64,1728]{1,0:T(8,128)S(1)}) custom-call(s32[1]{0:T(128)} %bitcast.row_ref.refs_0_, s32[1]{0:T(128)} %bitcast.1.owner_ref.refs_1_, s32[32,864]{1,0:T(8,128)S(1)} %bitcast.29, f32[32,864]{1,0:T(8,128)S(1)} %bitcast.24, f32[32,864]{1,0:T(8,128)S(1)} %bitcast.27, ...), custom_call_target="tpu_custom_call" | custom-call | flops 1146617856 | bytes 11943936 | tf_op jit(solution)/shard_map/product/pallas_call | solution.py:163
  11.7 15.6 %all_to_all.40.g_ref = f32[16,4,864]{2,1,0:T(4,128)S(1)} all-to-all(f32[16,4,864]{2,1,0:T(4,128)S(1)} %get-tuple-element.17), channel_id=1, replica_groups=mesh['freq'=16,'row'=2] {'freq'}, dimensions={0} | all-to-all | bytes 442368 | tf_op jit(solution)/shard_map/all_to_all | solution.py:320
  27.4 0.0 copy-done
  27.4 0.4 window.4
  27.8 16.3 %all_to_all.41.refs_0_ = f32[32,4,864]{2,1,0:T(4,128)S(1)} all-to-all(f32[32,4,864]{2,1,0:T(4,128)S(1)} %window.4), channel_id=1, replica_groups=mesh['freq'=16,'row'=2] {'freq','row'}, dimensions={0} | all-to-all | bytes 884736 | tf_op jit(solution)/shard_map/all_to_all | solution.py:323
  44.0 2.0 %product.5 = f32[16,4,864]{2,1,0:T(4,128)S(1)} custom-call(f32[32,4,864]{2,1,0:T(4,128)S(1)} %all_to_all.41.refs_0_, bf16[1728,1536]{1,0:T(8,128)(2,1)S(1)} %get-tuple-element.14.refs_7_.refs_1_.refs_2_, bf16[1728,1536]{1,0:T(8,128)(2,1)S(1)} %get-tuple-element.15.refs_8_.refs_2_.refs_3_, bf16[1728,512]{1,0:T(8,128)(2,1)S(1)} %get-tuple-element.16.refs_9_.refs_3_.refs_4_), custom_call_target="tpu_custom_call" | custom-call | flops 1146617856 | bytes 11943936 | tf_op jit(solution)/shard_map/product/pallas_call | solution.py:163
  46.0 13.0 %all_to_all.42.g_ref = f32[16,4,864]{2,1,0:T(4,128)S(1)} all-to-all(f32[16,4,864]{2,1,0:T(4,128)S(1)} %product.5), channel_id=1, replica_groups=mesh['freq'=16,'row'=2] {'freq'}, dimensions={0} | all-to-all | bytes 442368 | tf_op jit(solution)/shard_map/all_to_all | solution.py:320
  59.1 0.4 window.5
  59.5 16.0 %all_to_all.43.refs_0_ = f32[32,4,864]{2,1,0:T(4,128)S(1)} all-to-all(f32[32,4,864]{2,1,0:T(4,128)S(1)} %window.5), channel_id=1, replica_groups=mesh['freq'=16,'row'=2] {'freq','row'}, dimensions={0} | all-to-all | bytes 884736 | tf_op jit(solution)/shard_map/all_to_all | solution.py:323
  75.5 2.0 %product.6 = f32[16,4,864]{2,1,0:T(4,128)S(1)} custom-call(f32[32,4,864]{2,1,0:T(4,128)S(1)} %all_to_all.43.refs_0_, f32[64,1728]{1,0:T(8,128)S(1)} %get-tuple-element.19.refs_1_, bf16[1728,1536]{1,0:T(8,128)(2,1)S(1)} %get-tuple-element.14.refs_7_.refs_1_.refs_2_, bf16[1728,1536]{1,0:T(8,128)(2,1)S(1)} %get-tuple-element.15.refs_8_.refs_2_.refs_3_, ...), custom_call_target="tpu_custom_call" | custom-call | flops 1146617856 | bytes 11943936 | tf_op jit(solution)/shard_map/product/pallas_call | solution.py:163
  77.5 13.0 %all_to_all.44.g_ref = f32[16,4,864]{2,1,0:T(4,128)S(1)} all-to-all(f32[16,4,864]{2,1,0:T(4,128)S(1)} %product.6), channel_id=1, replica_groups=mesh['freq'=16,'row'=2] {'freq'}, dimensions={0} | all-to-all | bytes 442368 | tf_op jit(solution)/shard_map/all_to_all | solution.py:320
  90.5 0.4 window.6
  90.9 16.0 %all_to_all.45.refs_0_.minus_ref = f32[32,4,864]{2,1,0:T(4,128)S(1)} all-to-all(f32[32,4,864]{2,1,0:T(4,128)S(1)} %window.6), channel_id=1, replica_groups=mesh['freq'=16,'row'=2] {'freq','row'}, dimensions={0} | all-to-all | bytes 884736 | tf_op jit(solution)/shard_map/all_to_all | solution.py:323
  106.9 2.0 %product.7 = f32[16,4,864]{2,1,0:T(4,128)S(1)} custom-call(f32[32,4,864]{2,1,0:T(4,128)S(1)} %all_to_all.45.refs_0_.minus_ref, bf16[1728,1536]{1,0:T(8,128)(2,1)S(1)} %get-tuple-element.14.refs_7_.refs_1_.refs_2_, bf16[1728,1536]{1,0:T(8,128)(2,1)S(1)} %get-tuple-element.15.refs_8_.refs_2_.refs_3_, ...), custom_call_target="tpu_custom_call" | custom-call | flops 1146617856 | bytes 11943936 | tf_op jit(solution)/shard_map/product/pallas_call | solution.py:163
  108.9 13.0 %all_to_all.46.g_ref = f32[16,4,864]{2,1,0:T(4,128)S(1)} all-to-all(f32[16,4,864]{2,1,0:T(4,128)S(1)} %product.7), channel_id=1, replica_groups=mesh['freq'=16,'row'=2] {'freq'}, dimensions={0} | all-to-all | bytes 442368 | tf_op jit(solution)/shard_map/all_to_all | solution.py:320
  121.9 0.4 window.7
  122.3 12.1 %all_to_all.47.update_ref = f32[16,4,864]{2,1,0:T(4,128)S(1)} all-to-all(f32[16,4,864]{2,1,0:T(4,128)S(1)} %window.7), channel_id=1, replica_groups=mesh['freq'=16,'row'=2] {'freq'}, dimensions={0} | all-to-all | bytes 442368 | tf_op jit(solution)/shard_map/all_to_all | solution.py:323
  134.4 0.9 finish.1
Async XLA Ops:
  0.6 8.8 %collective-permute-start = (f32[32,864]{1,0:T(8,128)}, f32[32,864]{1,0:T(8,128)S(1)}, u32[]{:S(2)}, u32[]{:S(2)}) collective-permute-start(f32[32,864]{1,0:T(8,128)} %bitcast.23), channel_id=1, source_target_pairs={{0,1},{1,0},{2,3},{3,2},{4,5},{5,4},{6,7},{7,6},{8,9},{9,8},{10,11... | collective-permute-start | bytes 331784 | tf_op jit(solution)/shard_map/ppermute | solution.py:330
  3.7 5.8 %collective-permute-start.1 = (f32[32,864]{1,0:T(8,128)}, f32[32,864]{1,0:T(8,128)S(1)}, u32[]{:S(2)}, u32[]{:S(2)}) collective-permute-start(f32[32,864]{1,0:T(8,128)} %bitcast.26), channel_id=1, source_target_pairs={{0,1},{1,0},{2,3},{3,2},{4,5},{5,4},{6,7},{7,6},{8,9},{9,8},{10,11... | collective-permute-start | bytes 331784 | tf_op jit(solution)/shard_map/ppermute | solution.py:330
  3.8 5.7 %copy-start.1 = (f32[1,864,32]{1,2,0:T(8,128)S(1)}, f32[1,864,32]{1,2,0:T(8,128)}, u32[]{:S(2)}) copy-start(f32[1,864,32]{1,2,0:T(8,128)} %param.11) | copy-start | bytes 331780
  3.8 5.7 %copy-start.2 = (f32[1,864,32]{1,2,0:T(8,128)S(1)}, f32[1,864,32]{1,2,0:T(8,128)}, u32[]{:S(2)}) copy-start(f32[1,864,32]{1,2,0:T(8,128)} %param.12) | copy-start | bytes 331780
  3.8 5.7 %copy-start.3 = (s32[864,32]{0,1:T(8,128)S(1)}, s32[864,32]{0,1:T(8,128)}, u32[]{:S(2)}) copy-start(s32[864,32]{0,1:T(8,128)} %param.13) | copy-start | bytes 331780
  9.5 17.8 %copy-start = (f32[32,8,128]{2,1,0:T(8,128)S(1)}, f32[32,8,128]{2,1,0:T(8,128)}, u32[]{:S(2)}) copy-start(f32[32,8,128]{2,1,0:T(8,128)} %constant.21.clone.table_ref) | copy-start | bytes 393220

commit v4 on v3

--- a/solution.py
+++ b/solution.py
@@ -40,7 +40,7 @@
     return [whole_pieces] * 2 + ([rest] if rest else [])
 
 
-def prepare_body(bands, row_ref, owner_ref, re_ref, im_ref, *refs):
+def prepare_body(bands, rest, row_ref, owner_ref, re_ref, im_ref, *refs):
     *outs, re_held, im_held, arrived = refs
     half, full = re_ref.shape
     pairs = ((re_ref, re_held), (im_ref, im_held))
@@ -56,13 +56,13 @@
         for which, (_, held) in enumerate(pairs):
             copies[at, which].wait()
             first = start // TILE * TILE
-            if first + TILE <= half:
+            if not rest:
                 place = 2 * first + which * TILE + start - first
                 targets = [(outs[0], place), (outs[1], place)]
             else:
                 width = up(half - first, LANES)
                 place = which * width + start - first
-                targets = [(outs[2], place), (outs[2], place + 2 * width)]
+                targets = [(outs[0], place), (outs[0], place + 2 * width)]
             for line in range(0, full, LANES):
                 rows = slice(line, min(line + LANES, full))
                 parts = split(held[start : start + size, rows].T)
@@ -70,12 +70,15 @@
                     target[rows, place : place + size] = part
 
 
-def prepare(row, owner, reflect_re, reflect_im):
+def prepare(row, owner, reflect_re, reflect_im, rest):
     half, full = reflect_re.shape
-    bands = [(start, min(LANES, half - start)) for start in range(0, half, LANES)]
-    shapes = [jax.ShapeDtypeStruct((full, width), jnp.bfloat16) for width in columns_of(half)]
+    edge = half // TILE * TILE
+    span = range(edge, half, LANES) if rest else range(0, edge, LANES)
+    bands = [(start, min(LANES, half - start)) for start in span]
+    widths = columns_of(half)[2:] if rest else columns_of(half)[:2]
+    shapes = [jax.ShapeDtypeStruct((full, width), jnp.bfloat16) for width in widths]
     return pl.pallas_call(
-        functools.partial(prepare_body, bands),
+        functools.partial(prepare_body, bands, rest),
         in_specs=[whole(SMEM)] * 2 + [whole(pltpu.HBM)] * 2,
         out_specs=[whole(VMEM)] * len(shapes),
         out_shape=shapes,
@@ -84,7 +87,7 @@
             pltpu.VMEM((half, full), jnp.float32),
             pltpu.SemaphoreType.DMA((len(bands), 2)),
         ],
-        compiler_params=pltpu.CompilerParams(vmem_limit_bytes=40 << 20),
+        compiler_params=pltpu.CompilerParams(vmem_limit_bytes=(48 if rest else 40) << 20),
         cost_estimate=pl.CostEstimate(
             flops=32 * half * full * LANES, bytes_accessed=8 * half * full, transcendentals=0
         ),
@@ -331,9 +334,15 @@
 
     window = window_small if owners <= 32 else window_large
     bases = [focus_re[0].T, focus_im[0].T]
+    moved = [shift(bases[0], by) for by in range(1, shards)]
+    matrix = (reflect_re[0], reflect_im[0])
+    left, held = [], bases[1]
+    if half % TILE:
+        left = list(prepare(row, owner, *matrix, True))
+        held, left[0] = lax.optimization_barrier((held, left[0]))
     for by in range(1, shards):
-        bases += [shift(part, by) for part in bases[:2]]
-    weights = list(prepare(row, owner, reflect_re[0], reflect_im[0]))
+        bases += [moved[by - 1], shift(held, by)]
+    weights = list(prepare(row, owner, *matrix, False)) + left
 
     before, adds = [row, owner, first_arrival.T] + bases, None
     for section in range(ITERS):

time: 136 us -> 137 us (level)
    pallas_call x1 -> x2, Pallas kernels: 5.67 us -> 6.75 us  [prepare(): pl.pallas_call(functools.partial(prepare_body, bands, rest), in_specs=[wh...]
  transfers between devices with their start and end apart: 2 -> 2, of which waited for: 0 -> 0; matrix products, arithmetic and copies ran while one was open for 0% -> 0% of each run, Pallas kernels for 4% -> 5%
where the time goes in v4:
time: 137 us; the launch traced here: 136 us
  blocking collectives  115 us (84%)
  Pallas kernels  17.5 us (13%)
  starting transfers between devices  3.16 us (2%)
    all_to_all x4, blocking collectives, from_owners(): value = lax.all_to_all(value, axes, 0, 0, tiled=True)  60.4 us
    all_to_all x4, blocking collectives, to_owners(): return lax.all_to_all(value, 'freq', 0, 0, tiled=True)  54.7 us
    pallas_call x4, Pallas kernels, product(): pl.pallas_call(functools.partial(product_body, sign, points, shards, firs...  8.21 us
    pallas_call x2, Pallas kernels, prepare(): pl.pallas_call(functools.partial(prepare_body, bands, rest), in_specs=[wh...  6.75 us
    ppermute x2, starting transfers between devices, shift(): lax.ppermute(value, 'row', [(i, (i - by) % shards) for i in range(shards)])  3.16 us
  transfers between devices with their start and end apart: 2, of which 0 were waited for; matrix products, arithmetic and copies ran while one was open for 0% of the time, Pallas kernels for 5%

profile of v4, /device:TPU:0, one launch (start us, length us, event | category | flops | bytes accessed | tf_op | source)
XLA Modules:
  0.0 136.5 jit_solution(4040647141055660418)
XLA Ops:
  0.6 3.1 %collective-permute-start = (f32[32,864]{1,0:T(8,128)}, f32[32,864]{1,0:T(8,128)S(1)}, u32[]{:S(2)}, u32[]{:S(2)}) collective-permute-start(f32[32,864]{1,0:T(8,128)} %bitcast.23), channel_id=1, source_target_pairs={{0,1},{1,0},{2,3},{3,2},{4,5},{5,4},{6,7},{7,6},{8,9},{9,8},{10,11... | collective-permute-start | bytes 331784 | tf_op jit(solution)/shard_map/ppermute | solution.py:333
  3.7 0.0 copy-start.2
  3.7 1.8 %prepare.2.refs_9_.refs_3_.refs_4_ = bf16[1728,512]{1,0:T(8,128)(2,1)S(1)} custom-call(s32[1]{0:T(128)} %bitcast.row_ref.refs_0_, s32[1]{0:T(128)} %bitcast.1.owner_ref.refs_1_, f32[864,1728]{1,0:T(8,128)} %bitcast.30, f32[864,1728]{1,0:T(8,128)} %bitcast.32), custom_call_target="tpu_custom_call" | custom-call | flops 6115295232 | bytes 11943936 | tf_op jit(solution)/shard_map/prepare/pallas_call | solution.py:80
  5.5 0.0 copy-done.2
  5.5 0.0 copy-start.1
  5.5 0.0 copy-start.3
  5.5 0.1 collective-permute-start.1
  5.6 5.0 %prepare.3 = (bf16[1728,1536]{1,0:T(8,128)(2,1)S(1)}, bf16[1728,1536]{1,0:T(8,128)(2,1)S(1)}) custom-call(s32[1]{0:T(128)} %bitcast.row_ref.refs_0_, s32[1]{0:T(128)} %bitcast.1.owner_ref.refs_1_, f32[864,1728]{1,0:T(8,128)} %bitcast.31, f32[864,1728]{1,0:T(8,128)} %bitcast.33), custom_call_target="tpu_custom_call" | custom-call | flops 6115295232 | bytes 11943936 | tf_op jit(solution)/shard_map/prepare/pallas_call | solution.py:80
  10.6 0.0 collective-permute-done.refs_5_
  10.6 0.0 collective-permute-done.1.refs_6_
  10.6 0.0 copy-done.1
  10.6 0.0 copy-done.3
  10.6 0.0 copy-start
  10.6 2.2 %product.4 = (f32[16,4,864]{2,1,0:T(4,128)S(1)}, s32[4,864]{1,0:T(4,128)S(1)}, f32[64,1728]{1,0:T(8,128)S(1)}) custom-call(s32[1]{0:T(128)} %bitcast.row_ref.refs_0_, s32[1]{0:T(128)} %bitcast.1.owner_ref.refs_1_, s32[32,864]{1,0:T(8,128)S(1)} %bitcast.29, f32[32,864]{1,0:T(8,128)S(1)} %bitcast.24, f32[32,864]{1,0:T(8,128)S(1)} %bitcast.27, ...), custom_call_target="tpu_custom_call" | custom-call | flops 1146617856 | bytes 11943936 | tf_op jit(solution)/shard_map/product/pallas_call | solution.py:166
  12.9 15.7 %all_to_all.40.g_ref = f32[16,4,864]{2,1,0:T(4,128)S(1)} all-to-all(f32[16,4,864]{2,1,0:T(4,128)S(1)} %get-tuple-element.19), channel_id=1, replica_groups=mesh['freq'=16,'row'=2] {'freq'}, dimensions={0} | all-to-all | bytes 442368 | tf_op jit(solution)/shard_map/all_to_all | solution.py:323
  28.5 0.0 copy-done
  28.5 0.4 window.4
  28.9 16.3 %all_to_all.41.refs_0_ = f32[32,4,864]{2,1,0:T(4,128)S(1)} all-to-all(f32[32,4,864]{2,1,0:T(4,128)S(1)} %window.4), channel_id=1, replica_groups=mesh['freq'=16,'row'=2] {'freq','row'}, dimensions={0} | all-to-all | bytes 884736 | tf_op jit(solution)/shard_map/all_to_all | solution.py:326
  45.2 2.0 %product.5 = f32[16,4,864]{2,1,0:T(4,128)S(1)} custom-call(f32[32,4,864]{2,1,0:T(4,128)S(1)} %all_to_all.41.refs_0_, bf16[1728,1536]{1,0:T(8,128)(2,1)S(1)} %get-tuple-element.16.refs_7_.refs_1_.refs_2_, bf16[1728,1536]{1,0:T(8,128)(2,1)S(1)} %get-tuple-element.17.refs_8_.refs_2_.refs_3_, bf16[1728,512]{1,0:T(8,128)(2,1)S(1)} %prepare.2.refs_9_.refs_3_.refs_4_), custom_call_target="tpu_custom_call" | custom-call | flops 1146617856 | bytes 11943936 | tf_op jit(solution)/shard_map/product/pallas_call | solution.py:166
  47.2 13.0 %all_to_all.42.g_ref = f32[16,4,864]{2,1,0:T(4,128)S(1)} all-to-all(f32[16,4,864]{2,1,0:T(4,128)S(1)} %product.5), channel_id=1, replica_groups=mesh['freq'=16,'row'=2] {'freq'}, dimensions={0} | all-to-all | bytes 442368 | tf_op jit(solution)/shard_map/all_to_all | solution.py:323
  60.2 0.4 window.5
  60.6 16.0 %all_to_all.43.refs_0_ = f32[32,4,864]{2,1,0:T(4,128)S(1)} all-to-all(f32[32,4,864]{2,1,0:T(4,128)S(1)} %window.5), channel_id=1, replica_groups=mesh['freq'=16,'row'=2] {'freq','row'}, dimensions={0} | all-to-all | bytes 884736 | tf_op jit(solution)/shard_map/all_to_all | solution.py:326
  76.6 2.0 %product.6 = f32[16,4,864]{2,1,0:T(4,128)S(1)} custom-call(f32[32,4,864]{2,1,0:T(4,128)S(1)} %all_to_all.43.refs_0_, f32[64,1728]{1,0:T(8,128)S(1)} %get-tuple-element.21.refs_1_, bf16[1728,1536]{1,0:T(8,128)(2,1)S(1)} %get-tuple-element.16.refs_7_.refs_1_.refs_2_, bf16[1728,1536]{1,0:T(8,128)(2,1)S(1)} %get-tuple-element.17.refs_8_.refs_2_.refs_3_, ...), custom_call_target="tpu_custom_call" | custom-call | flops 1146617856 | bytes 11943936 | tf_op jit(solution)/shard_map/product/pallas_call | solution.py:166
  78.7 13.0 %all_to_all.44.g_ref = f32[16,4,864]{2,1,0:T(4,128)S(1)} all-to-all(f32[16,4,864]{2,1,0:T(4,128)S(1)} %product.6), channel_id=1, replica_groups=mesh['freq'=16,'row'=2] {'freq'}, dimensions={0} | all-to-all | bytes 442368 | tf_op jit(solution)/shard_map/all_to_all | solution.py:323
  91.7 0.4 window.6
  92.1 16.0 %all_to_all.45.refs_0_.minus_ref = f32[32,4,864]{2,1,0:T(4,128)S(1)} all-to-all(f32[32,4,864]{2,1,0:T(4,128)S(1)} %window.6), channel_id=1, replica_groups=mesh['freq'=16,'row'=2] {'freq','row'}, dimensions={0} | all-to-all | bytes 884736 | tf_op jit(solution)/shard_map/all_to_all | solution.py:326
  108.1 2.0 %product.7 = f32[16,4,864]{2,1,0:T(4,128)S(1)} custom-call(f32[32,4,864]{2,1,0:T(4,128)S(1)} %all_to_all.45.refs_0_.minus_ref, bf16[1728,1536]{1,0:T(8,128)(2,1)S(1)} %get-tuple-element.16.refs_7_.refs_1_.refs_2_, bf16[1728,1536]{1,0:T(8,128)(2,1)S(1)} %get-tuple-element.17.refs_8_.refs_2_.refs_3_, bf16[1728,512]{1,0:T(8,128)(2,1)S(1)} %prepare.2.refs_9_.refs_3_.refs_4_), custom_call_target="tpu_custom_call" | custom-call | flops 1146617856 | bytes 11943936 | tf_op jit(solution)/shard_map/product/pallas_call | solution.py:166
  110.1 13.0 %all_to_all.46.g_ref = f32[16,4,864]{2,1,0:T(4,128)S(1)} all-to-all(f32[16,4,864]{2,1,0:T(4,128)S(1)} %product.7), channel_id=1, replica_groups=mesh['freq'=16,'row'=2] {'freq'}, dimensions={0} | all-to-all | bytes 442368 | tf_op jit(solution)/shard_map/all_to_all | solution.py:323
  123.1 0.4 window.7
  123.5 12.1 %all_to_all.47.update_ref = f32[16,4,864]{2,1,0:T(4,128)S(1)} all-to-all(f32[16,4,864]{2,1,0:T(4,128)S(1)} %window.7), channel_id=1, replica_groups=mesh['freq'=16,'row'=2] {'freq'}, dimensions={0} | all-to-all | bytes 442368 | tf_op jit(solution)/shard_map/all_to_all | solution.py:326
  135.6 0.9 finish.1
Async XLA Ops:
  0.6 10.0 %collective-permute-start = (f32[32,864]{1,0:T(8,128)}, f32[32,864]{1,0:T(8,128)S(1)}, u32[]{:S(2)}, u32[]{:S(2)}) collective-permute-start(f32[32,864]{1,0:T(8,128)} %bitcast.23), channel_id=1, source_target_pairs={{0,1},{1,0},{2,3},{3,2},{4,5},{5,4},{6,7},{7,6},{8,9},{9,8},{10,11... | collective-permute-start | bytes 331784 | tf_op jit(solution)/shard_map/ppermute | solution.py:333
  3.7 1.8 %copy-start.2 = (f32[1,864,32]{1,2,0:T(8,128)S(1)}, f32[1,864,32]{1,2,0:T(8,128)}, u32[]{:S(2)}) copy-start(f32[1,864,32]{1,2,0:T(8,128)} %param.12) | copy-start | bytes 331780
  5.5 5.1 %copy-start.1 = (f32[1,864,32]{1,2,0:T(8,128)S(1)}, f32[1,864,32]{1,2,0:T(8,128)}, u32[]{:S(2)}) copy-start(f32[1,864,32]{1,2,0:T(8,128)} %param.11) | copy-start | bytes 331780
  5.5 5.1 %copy-start.3 = (s32[864,32]{0,1:T(8,128)S(1)}, s32[864,32]{0,1:T(8,128)}, u32[]{:S(2)}) copy-start(s32[864,32]{0,1:T(8,128)} %param.13) | copy-start | bytes 331780
  5.5 5.1 %collective-permute-start.1 = (f32[32,864]{1,0:T(8,128)S(1)}, f32[32,864]{1,0:T(8,128)S(1)}, u32[]{:S(2)}, u32[]{:S(2)}) collective-permute-start(f32[32,864]{1,0:T(8,128)S(1)} %bitcast.26), channel_id=1, source_target_pairs={{0,1},{1,0},{2,3},{3,2},{4,5},{5,4},{6,7},{7,6},{8,9},{9,8},{10,11... | collective-permute-start | bytes 331784 | tf_op jit(solution)/shard_map/ppermute | solution.py:333
  10.6 17.9 %copy-start = (f32[32,8,128]{2,1,0:T(8,128)S(1)}, f32[32,8,128]{2,1,0:T(8,128)}, u32[]{:S(2)}) copy-start(f32[32,8,128]{2,1,0:T(8,128)} %constant.21.clone.table_ref) | copy-start | bytes 393220
